TPU v7x, 8 devices: a whole 2x2x1 slice. The times are simulated.
8 devices in a mesh: rep: 1 (over z), dp: 8 (over y, x, core).
Axes of the slice: x: 2, y: 2, z: 1, core: 2. Of those that a mesh axis runs over, the one named last changes fastest.
Arguments:
- hidden: bfloat16 [256, 2048], P(('rep', 'dp'))
- lengths: int32 [256], P(('rep', 'dp'))
- kv_cache: bfloat16 [2, 256, 512, 576], P(None, ('rep', 'dp'))
- norm_attn: float32 [2, 2048], replicated
- w_q: bfloat16 [2, 2048, 9216], replicated
- w_o: bfloat16 [2, 8192, 2048], replicated
- norm_ffn: float32 [2, 2048], replicated
- w_gate: bfloat16 [2, 2048, 10944], P(None, None, 'dp')
- w_up: bfloat16 [2, 2048, 10944], P(None, None, 'dp')
- w_down: bfloat16 [2, 10944, 2048], P(None, 'dp')
- norm_final: float32 [2048], replicated
- w_head: bfloat16 [2048, 102400], P(None, 'dp')
Outputs:
- output: float32 [256, 102400], P('rep', 'dp')
All inputs are finite; a program needn't handle non-finite values.
Results may differ from a plain program's by a relative error of at most 0.02.
Values are sent between devices in bfloat16 or wider.
A program may use at most 1.25 GiB of HBM per device.

v0:
```python
import jax
import jax.numpy as jnp
from jax import lax
from jax.sharding import PartitionSpec as P

LATENT_DIM = 512
QK_SCALE = 192 ** -0.5
NORM_EPS = 1e-6


def rms_norm(x_rows, gain_vec):
    x_float = x_rows.astype(jnp.float32)
    inv_rms = lax.rsqrt(jnp.mean(x_float * x_float, axis=-1, keepdims=True) + NORM_EPS)
    return (x_float * inv_rms * gain_vec).astype(jnp.bfloat16)


def mla_attention(normed, w_q, kv_cache, lengths):
    num_rows, seq_len, kv_width = kv_cache.shape
    q_heads = jnp.dot(normed, w_q, preferred_element_type=jnp.float32).astype(jnp.bfloat16)
    q_heads = q_heads.reshape(num_rows, -1, kv_width)
    scores = jnp.einsum('bhc,btc->bht', q_heads, kv_cache, preferred_element_type=jnp.float32) * QK_SCALE
    key_pos = lax.broadcasted_iota(jnp.int32, (1, 1, seq_len), 2)
    scores = jnp.where(key_pos < lengths[:, None, None], scores, -1e30)
    attn_probs = jax.nn.softmax(scores, axis=-1).astype(jnp.bfloat16)
    context = jnp.einsum('bht,btc->bhc', attn_probs, kv_cache[:, :, :LATENT_DIM], preferred_element_type=jnp.float32)
    return context.astype(jnp.bfloat16).reshape(num_rows, -1)


def ffn_block(normed, w_gate, w_up, w_down):
    gate_proj = jnp.dot(normed, w_gate, preferred_element_type=jnp.float32)
    up_proj = jnp.dot(normed, w_up, preferred_element_type=jnp.float32)
    act_rows = (jax.nn.silu(gate_proj) * up_proj).astype(jnp.bfloat16)
    return jnp.dot(act_rows, w_down, preferred_element_type=jnp.float32)


def add_residual(x_rows, delta):
    return (x_rows.astype(jnp.float32) + delta).astype(jnp.bfloat16)


def solution(mesh):
    row_axes = ('rep', 'dp')
    specs_in = (P(row_axes, None), P(row_axes), P(None, row_axes, None, None), P(), P(), P(), P(),
                P(None, None, 'dp'), P(None, None, 'dp'), P(None, 'dp', None), P(), P(None, 'dp'))

    def device_step(hidden, lengths, kv_cache, norm_attn, w_q, w_o, norm_ffn, w_gate, w_up, w_down, norm_final, w_head):
        x_rows = hidden
        for layer_idx in range(kv_cache.shape[0]):
            normed = rms_norm(x_rows, norm_attn[layer_idx])
            context = mla_attention(normed, w_q[layer_idx], kv_cache[layer_idx], lengths)
            x_rows = add_residual(x_rows, jnp.dot(context, w_o[layer_idx], preferred_element_type=jnp.float32))
            normed = rms_norm(x_rows, norm_ffn[layer_idx])
            gathered = lax.all_gather(normed, 'dp', axis=0, tiled=True)
            part_sum = ffn_block(gathered, w_gate[layer_idx], w_up[layer_idx], w_down[layer_idx])
            ffn_out = lax.psum_scatter(part_sum, 'dp', scatter_dimension=0, tiled=True)
            x_rows = add_residual(x_rows, ffn_out)
        normed = rms_norm(x_rows, norm_final)
        gathered = lax.all_gather(normed, 'dp', axis=0, tiled=True)
        return jnp.dot(gathered, w_head, preferred_element_type=jnp.float32)

    return jax.shard_map(device_step, mesh=mesh, in_specs=specs_in, out_specs=P('rep', 'dp'), check_vma=False)
```

profile of v0, /device:TPU:0, one launch (start us, length us, event | category | flops | bytes accessed | tf_op | source)
XLA Modules:
  0.0 319.0 jit_solution(11398899945515460008)
XLA Ops:
  6.5 0.8 fusion.108
  7.3 1.0 fusion.93
  8.4 15.2 %fusion.18 = bf16[32,9216]{1,0:T(8,128)(2,1)S(1)} fusion(bf16[2,2048,9216]{2,1,0:T(8,128)(2,1)} %param.16, bf16[32,2048]{1,0:T(8,128)(2,1)} %param.12, f32[2048]{0:T(1024)S(1)} %bitcast.97, f32[32]{0:T(128)S(1)} %add_rsqrt_fusion.4), kind=kOutput, calls=%fused_computation.20 | convolution fusion | flops 1208516608 | bytes 38477952 | tf_op jit(solution)/shard_map/dot_general | solution.py:19
  24.3 25.4 %slice_bitcast_fusion.1 = (bf16[32,512,576]{1,2,0:T(8,128)(2,1)}, bf16[32,512,576]{1,2,0:T(8,128)(2,1)}) fusion(bf16[2,32,512,576]{2,3,1,0:T(8,128)(2,1)} %param.14), kind=kLoop, calls=%fused_computation.15 | loop fusion | bytes 75497472 | tf_op jit(solution)/shard_map/squeeze | solution.py:49
  49.7 8.0 %fusion.109 = (f32[32,16]{1,0:T(8,128)S(1)}, f32[32,16,512]{2,1,0:T(8,128)S(1)}) fusion(bf16[32,16,576]{2,1,0:T(8,128)(2,1)S(1)} %reshape.78, pred[32,512]{1,0:T(8,128)(4,1)S(1)} %iota_compare_fusion, bf16[2,32,512,576]{2,3,1,0:T(8,128)(2,1)} %param.14), kind=kOutput, calls=%fused_computation.99 | convolution fusion | flops 303038976 | bytes 20531200 | tf_op jit(solution)/shard_map/sub | solution.py:24
  57.7 8.2 %fusion.78 = bf16[32,16,512]{2,1,0:T(8,128)(2,1)S(1)} fusion(bf16[32,512,576]{1,2,0:T(8,128)(2,1)} %get-tuple-element.9, f32[32,16,512]{2,1,0:T(8,128)S(1)} %get-tuple-element.16, f32[32,16]{1,0:T(8,128)S(1)} %get-tuple-element.15), kind=kOutput, calls=%fused_computation.58 | convolution fusion | flops 269221888 | bytes 18352128 | tf_op jit(solution)/shard_map/bht,btc->bhc/dot_general | solution.py:25
  66.2 13.7 %multiply_reduce_fusion.1 = (f32[32]{0:T(128)S(1)}, f32[32,2048]{1,0:T(8,128)S(1)}) fusion(bf16[32,8192]{1,0:T(8,128)(2,1)S(1)} %bitcast.92, bf16[2,8192,2048]{2,1,0:T(8,128)(2,1)} %param.17, bf16[32,2048]{1,0:T(8,128)(2,1)S(1)} %copy-done), kind=kOutput, calls=%fused_computation.84 | convolution fusion | flops 1074135040 | bytes 34472064 | tf_op jit(solution)/shard_map/dot_general | solution.py:50
  81.0 20.3 %all-gather.4.cloned.1.call-done = bf16[256,2048]{1,0:T(8,128)(2,1)} async-done(((bf16[32,2048]{1,0:T(8,128)(2,1)}), bf16[256,2048]{1,0:T(8,128)(2,1)}) %all-gather.4.cloned.1.call-update) | async-done | bytes 1048592 | tf_op jit(solution)/shard_map/all_gather | solution.py:52
  101.3 4.6 %fusion.34 = f32[256,1368]{0,1:T(8,128)S(1)} fusion(bf16[256,2048]{1,0:T(8,128)(2,1)} %all-gather.4.cloned.1.call-done, bf16[2,2048,1368]{1,2,0:T(8,128)(2,1)} %param.19), kind=kOutput, calls=%fused_computation.32 | convolution fusion | flops 1434451968 | bytes 8052736 | tf_op jit(solution)/shard_map/dot_general | solution.py:30
  105.9 12.0 %fusion.30 = f32[256,2048]{1,0:T(8,128)} fusion(bf16[2,1368,2048]{2,1,0:T(8,128)(2,1)} %param.21, bf16[256,2048]{1,0:T(8,128)(2,1)} %all-gather.4.cloned.1.call-done, bf16[2,2048,1368]{1,2,0:T(8,128)(2,1)} %param.20, f32[256,1368]{0,1:T(8,128)S(1)} %fusion.34), kind=kOutput, calls=%fused_computation.28 | convolution fusion | flops 2871005184 | bytes 15753216 | tf_op jit(solution)/shard_map/dot_general | solution.py:33
  118.2 32.4 %reduce-scatter.3.cloned.1.call-done = f32[32,2048]{1,0:T(8,128)} async-done(((f32[256,2048]{1,0:T(8,128)}), f32[32,2048]{1,0:T(8,128)}) %reduce-scatter.3.cloned.1.call-update) | async-done | bytes 262160 | tf_op jit(solution)/shard_map/reduce_scatter | solution.py:54
  150.7 1.1 fusion.96
  151.8 15.2 %fusion.21 = bf16[32,9216]{1,0:T(8,128)(2,1)S(1)} fusion(bf16[2,2048,9216]{2,1,0:T(8,128)(2,1)} %param.16, bf16[32,2048]{1,0:T(8,128)(2,1)S(1)} %get-tuple-element.8, f32[2048]{0:T(1024)S(1)} %bitcast.96, f32[32]{0:T(128)S(1)} %add_rsqrt_fusion.2), kind=kOutput, calls=%fused_computation.21 | convolution fusion | flops 1208516608 | bytes 38477952 | tf_op jit(solution)/shard_map/dot_general | solution.py:19
  167.6 8.0 %fusion.110 = (f32[32,16]{1,0:T(8,128)S(1)}, f32[32,16,512]{2,1,0:T(8,128)S(1)}) fusion(bf16[32,16,576]{2,1,0:T(8,128)(2,1)S(1)} %reshape.80, pred[32,512]{1,0:T(8,128)(4,1)S(1)} %iota_compare_fusion, bf16[2,32,512,576]{2,3,1,0:T(8,128)(2,1)} %param.14), kind=kOutput, calls=%fused_computation.100 | convolution fusion | flops 303038976 | bytes 20531200 | tf_op jit(solution)/shard_map/sub | solution.py:24
  175.6 8.2 %fusion.81 = bf16[32,16,512]{2,1,0:T(8,128)(2,1)S(1)} fusion(bf16[32,512,576]{1,2,0:T(8,128)(2,1)} %get-tuple-element.10, f32[32,16,512]{2,1,0:T(8,128)S(1)} %get-tuple-element.20, f32[32,16]{1,0:T(8,128)S(1)} %get-tuple-element.19), kind=kOutput, calls=%fused_computation.59 | convolution fusion | flops 269221888 | bytes 18352128 | tf_op jit(solution)/shard_map/bht,btc->bhc/dot_general | solution.py:25
  184.1 13.7 %multiply_reduce_fusion = (f32[32]{0:T(128)S(1)}, f32[32,2048]{1,0:T(8,128)S(1)}) fusion(bf16[32,8192]{1,0:T(8,128)(2,1)S(1)} %bitcast.90, bf16[2,8192,2048]{2,1,0:T(8,128)(2,1)} %param.17, bf16[32,2048]{1,0:T(8,128)(2,1)S(1)} %get-tuple-element.8), kind=kOutput, calls=%fused_computation.81 | convolution fusion | flops 1074135040 | bytes 34472064 | tf_op jit(solution)/shard_map/dot_general | solution.py:50
  197.8 0.8 multiply_convert_fusion
  198.9 17.4 %all-gather.6.cloned.1.call-done = bf16[256,2048]{1,0:T(8,128)(2,1)} async-done(((bf16[32,2048]{1,0:T(8,128)(2,1)}), bf16[256,2048]{1,0:T(8,128)(2,1)}) %all-gather.6.cloned.1.call-update) | async-done | bytes 1048592 | tf_op jit(solution)/shard_map/all_gather | solution.py:52
  216.3 4.6 %fusion.28 = f32[256,1368]{0,1:T(8,128)S(1)} fusion(bf16[256,2048]{1,0:T(8,128)(2,1)} %all-gather.6.cloned.1.call-done, bf16[2,2048,1368]{1,2,0:T(8,128)(2,1)} %param.19), kind=kOutput, calls=%fused_computation.26 | convolution fusion | flops 1434451968 | bytes 8052736 | tf_op jit(solution)/shard_map/dot_general | solution.py:30
  220.9 12.1 %fusion.24 = f32[256,2048]{1,0:T(8,128)} fusion(bf16[2,1368,2048]{2,1,0:T(8,128)(2,1)} %param.21, bf16[256,2048]{1,0:T(8,128)(2,1)} %all-gather.6.cloned.1.call-done, bf16[2,2048,1368]{1,2,0:T(8,128)(2,1)} %param.20, f32[256,1368]{0,1:T(8,128)S(1)} %fusion.28), kind=kOutput, calls=%fused_computation.22 | convolution fusion | flops 2871005184 | bytes 15753216 | tf_op jit(solution)/shard_map/dot_general | solution.py:33
  233.1 32.7 %reduce-scatter.5.cloned.1.call-done = f32[32,2048]{1,0:T(8,128)} async-done(((f32[256,2048]{1,0:T(8,128)}), f32[32,2048]{1,0:T(8,128)}) %reduce-scatter.5.cloned.1.call-update) | async-done | bytes 262160 | tf_op jit(solution)/shard_map/reduce_scatter | solution.py:54
  265.8 1.1 fusion.90
  267.7 17.7 %all-gather.8.cloned.1.call-done = bf16[256,2048]{1,0:T(8,128)(2,1)} async-done(((bf16[32,2048]{1,0:T(8,128)(2,1)}), bf16[256,2048]{1,0:T(8,128)(2,1)}) %all-gather.8.cloned.1.call-update) | async-done | bytes 1048592 | tf_op jit(solution)/shard_map/all_gather | solution.py:57
  285.4 27.1 %fusion.111 = f32[256,12800]{1,0:T(8,128)} fusion(bf16[256,2048]{1,0:T(8,128)(2,1)} %all-gather.8.cloned.1.call-done, bf16[2048,12800]{1,0:T(8,128)(2,1)} %param.23), kind=kOutput, calls=%fused_computation.101 | convolution fusion | flops 13421772800 | bytes 66584576 | tf_op jit(solution)/shard_map/dot_general | solution.py:58
  (31 shorter events, 4.2 us)
Async XLA Ops:
  6.5 94.8 %all-gather.4.cloned.1.call-start = ((), (), s32[]{:S(2)}) async-start(), calls=%async_computation.2 | async-start | bytes 1179648 | tf_op jit(solution)/shard_map/all_gather | solution.py:52
  8.4 15.8 %copy-start.3 = (s32[32]{0:T(128)S(1)}, s32[32]{0:T(128)}, u32[]{:S(2)}) copy-start(s32[32]{0:T(128)} %param.13) | copy-start | bytes 388
  57.7 8.5 %copy-start = (bf16[32,2048]{1,0:T(8,128)(2,1)S(1)}, bf16[32,2048]{1,0:T(8,128)(2,1)}, u32[]{:S(2)}) copy-start(bf16[32,2048]{1,0:T(8,128)(2,1)} %param.12) | copy-start | bytes 393220
  66.2 13.7 %copy-start.1 = (f32[2,2048]{1,0:T(2,128)S(1)}, f32[2,2048]{1,0:T(2,128)}, u32[]{:S(2)}) copy-start(f32[2,2048]{1,0:T(2,128)} %param.18) | copy-start | bytes 49156
  80.8 69.9 %reduce-scatter.3.cloned.1.call-start = ((), (), s32[]{:S(2)}) async-start(), calls=%async_computation.3 | async-start | bytes 2359296 | tf_op jit(solution)/shard_map/reduce_scatter | solution.py:54
  118.0 98.3 %all-gather.6.cloned.1.call-start = ((), (), s32[]{:S(2)}) async-start(), calls=%async_computation.4 | async-start | bytes 1179648 | tf_op jit(solution)/shard_map/all_gather | solution.py:52
  198.5 67.3 %reduce-scatter.5.cloned.1.call-start = ((), (), s32[]{:S(2)}) async-start(), calls=%async_computation.5 | async-start | bytes 2359296 | tf_op jit(solution)/shard_map/reduce_scatter | solution.py:54
  220.9 46.0 %copy-start.2 = (f32[2048]{0:T(1024)S(1)}, f32[2048]{0:T(1024)}, u32[]{:S(2)}) copy-start(f32[2048]{0:T(1024)} %param.22) | copy-start | bytes 24580
  233.1 52.3 %all-gather.8.cloned.1.call-start = ((), (), s32[]{:S(2)}) async-start(), calls=%async_computation.6 | async-start | bytes 1179648 | tf_op jit(solution)/shard_map/all_gather | solution.py:57
Sparse Core Ops, SparseCore 0:
  80.9 20.3 all-gather.3
  118.1 32.5 reduce-scatter.2
  198.7 17.5 all-gather.5
  233.2 32.5 reduce-scatter.4
  267.8 17.5 all-gather.7
where the time goes:
time: 319 us
  matrix products  151 us (47%)
  waiting for transfers between devices  121 us (38%)
  local copies, waits for them, and re-layouts  27.9 us (9%)
  between operations  13.3 us (4%)
  other arithmetic  5.6 us (2%)
    reduce_scatter x2, waiting for transfers between devices, device_step(): ffn_out = lax.psum_scatter(part_sum, 'dp', scatter_dimension=0, tiled=True)  65.1 us
    all_gather x3, waiting for transfers between devices, device_step(): gathered = lax.all_gather(normed, 'dp', axis=0, tiled=True)  55.4 us
    dot_general x2, matrix products, mla_attention(): jnp.dot(normed, w_q, preferred_element_type=jnp.float32)  30.5 us
    dot_general x2, matrix products, device_step(): jnp.dot(context, w_o[layer_idx], preferred_element_type=jnp.float32)  27.4 us
    dot_general x1, matrix products, device_step(): return jnp.dot(gathered, w_head, preferred_element_type=jnp.float32)  27.1 us
    squeeze x1, local copies, waits for them, and re-layouts, device_step(): kv_cache[layer_idx]  25.4 us
    dot_general x2, matrix products, ffn_block(): return jnp.dot(act_rows, w_down, preferred_element_type=jnp.float32)  24.2 us
    dot_general x2, matrix products, mla_attention(): jnp.einsum('bht,btc->bhc', attn_probs, kv_cache[:, :, :LATENT_DIM], prefe...  16.4 us
  transfers between devices with their start and end apart: 5, of which 5 were waited for; matrix products, arithmetic and copies ran while one was open for 0% of the time, Pallas kernels for 0%

commit v1 on v0

v1 whole, which is shorter than its diff:
```python
import functools

import jax
import jax.numpy as jnp
from jax import lax
from jax.experimental import pallas as pl
from jax.experimental.pallas import tpu as pltpu
from jax.sharding import PartitionSpec as P

LATENT_DIM = 512
QK_SCALE = 192 ** -0.5
NORM_EPS = 1e-6
MESH_ID = pl.DeviceIdType.MESH
NUM_DEV = 8
RS_CHUNK = 512


def rms_norm(x_rows, gain_vec):
    x_float = x_rows.astype(jnp.float32)
    inv_rms = lax.rsqrt(jnp.mean(x_float * x_float, axis=-1, keepdims=True) + NORM_EPS)
    return (x_float * inv_rms * gain_vec).astype(jnp.bfloat16)


def mla_attention(normed, w_q, kv_cache, lengths):
    num_rows, seq_len, kv_width = kv_cache.shape
    q_heads = jnp.dot(normed, w_q, preferred_element_type=jnp.float32).astype(jnp.bfloat16)
    q_heads = q_heads.reshape(num_rows, -1, kv_width)
    scores = jnp.einsum('bhc,btc->bht', q_heads, kv_cache, preferred_element_type=jnp.float32) * QK_SCALE
    key_pos = lax.broadcasted_iota(jnp.int32, (1, 1, seq_len), 2)
    scores = jnp.where(key_pos < lengths[:, None, None], scores, -1e30)
    attn_probs = jax.nn.softmax(scores, axis=-1).astype(jnp.bfloat16)
    context = jnp.einsum('bht,btc->bhc', attn_probs, kv_cache[:, :, :LATENT_DIM], preferred_element_type=jnp.float32)
    return context.astype(jnp.bfloat16).reshape(num_rows, -1)


def add_residual(x_rows, delta):
    return (x_rows.astype(jnp.float32) + delta).astype(jnp.bfloat16)


def ffn_cuts(width):
    return [(lo, min(lo + 512, width)) for lo in range(0, width, 512)]


def peers():
    me = lax.axis_index('dp')
    core, x, y = me % 2, (me // 2) % 2, me // 4
    flip = lambda c, a, b: ((y + b) % 2) * 4 + ((x + a) % 2) * 2 + (core + c) % 2
    return me, {1: flip(1, 0, 0), 2: flip(0, 1, 0), 4: flip(0, 0, 1), 6: flip(0, 1, 1)}


def remote(src, dst, send, recv, dev):
    return pltpu.make_async_remote_copy(src_ref=src, dst_ref=dst, send_sem=send, recv_sem=recv,
                                        device_id={'dp': dev}, device_id_type=MESH_ID)


def ffn_kernel(layer, last, x_ref, gain_ref, gfin_ref, wg_hbm, wu_hbm, wd_hbm, *refs):
    if last:
        (out_ref, rows, wg, wu, wd, act, part, pair_in, total, chip_in, fin,
         w_sem, ag_send, ag_recv, pair_send, pair_recv, chip_send, chip_recv, fin_send, fin_recv) = refs
    else:
        (out_ref, rows, wg, wu, wd, act, part, pair_in, total, chip_in,
         w_sem, ag_send, ag_recv, pair_send, pair_recv, chip_send, chip_recv) = refs
    me, peer = peers()
    n_rows, d_model = x_ref.shape
    width = wg.shape[1]
    cuts = ffn_cuts(width)
    n_cuts, n_chunks = len(cuts), d_model // RS_CHUNK

    loads = []
    for i, (lo, hi) in enumerate(cuts):
        for j, (src, dst) in enumerate(((wg_hbm, wg), (wu_hbm, wu))):
            copy = pltpu.make_async_copy(src.at[layer, :, pl.ds(lo, hi - lo)], dst.at[:, pl.ds(lo, hi - lo)],
                                         w_sem.at[2 * i + j])
            copy.start()
            loads.append(copy)
    down_loads = []
    for c in range(n_chunks):
        cols = pl.ds(c * RS_CHUNK, RS_CHUNK)
        copy = pltpu.make_async_copy(wd_hbm.at[layer, :, cols], wd.at[:, cols], w_sem.at[2 * n_cuts + c])
        copy.start()
        down_loads.append(copy)

    rows[0] = rms_norm(x_ref[...], gain_ref[...])

    barrier = pltpu.get_barrier_semaphore()
    for j in (1, 2, 4, 6):
        pl.semaphore_signal(barrier, inc=1, device_id={'dp': peer[j]}, device_id_type=MESH_ID)
    pl.semaphore_wait(barrier, 4)

    sends = {j: remote(rows.at[0], rows.at[j], ag_send.at[j], ag_recv.at[j], peer[j]) for j in (6, 2, 4, 1)}
    for copy in sends.values():
        copy.start()
    for j in (2, 4, 6):
        sends[j].wait_recv()
        sends[j + 1] = remote(rows.at[j], rows.at[j + 1], ag_send.at[j + 1], ag_recv.at[j + 1], peer[1])
        sends[j + 1].start()
    for j in (1, 3, 5, 7):
        sends[j].wait_recv()

    for i, (lo, hi) in enumerate(cuts):
        cols = pl.ds(lo, hi - lo)
        loads[2 * i].wait()
        loads[2 * i + 1].wait()
        full = rows[...].reshape(NUM_DEV * n_rows, d_model)
        gate = jnp.dot(full, wg[:, cols], preferred_element_type=jnp.float32)
        up = jnp.dot(full, wu[:, cols], preferred_element_type=jnp.float32)
        act[:, cols] = (jax.nn.silu(gate) * up).astype(jnp.bfloat16)

    pair, chip = [], []

    def reduce_chunk(c):
        pair[c].wait_recv()
        for k in range(4):
            both = part[c, k, 0] + pair_in[c, k]
            if k == 0:
                part[c, 0, 0] = both
            else:
                total[c, k - 1] = both.astype(jnp.bfloat16)
        for k in (3, 1, 2):
            copy = remote(total.at[c, k - 1], chip_in.at[c, k - 1], chip_send.at[c, k - 1], chip_recv.at[c, k - 1],
                          peer[2 * k])
            copy.start()
            chip.append(copy)

    for c in range(n_chunks):
        down_loads[c].wait()
        y = jnp.dot(act[...], wd[:, pl.ds(c * RS_CHUNK, RS_CHUNK)], preferred_element_type=jnp.float32)
        part[c] = y.reshape(4, 2, n_rows, RS_CHUNK)
        copy = remote(part.at[c, :, 1], pair_in.at[c], pair_send.at[c], pair_recv.at[c], peer[1])
        copy.start()
        pair.append(copy)
        if c >= 1:
            reduce_chunk(c - 1)
    reduce_chunk(n_chunks - 1)

    for copy in chip:
        copy.wait_recv()
    x_new = []
    for c in range(n_chunks):
        cols = pl.ds(c * RS_CHUNK, RS_CHUNK)
        y = part[c, 0, 0]
        for k in range(3):
            y = y + chip_in[c, k].astype(jnp.float32)
        x_new.append((x_ref[:, cols].astype(jnp.float32) + y).astype(jnp.bfloat16))
    x_new = jnp.concatenate(x_new, axis=1)

    if last:
        fin[...] = rms_norm(x_new, gfin_ref[...])
        out_ref[me] = fin[...]
    else:
        out_ref[...] = x_new

    for copy in list(sends.values()) + pair + chip:
        copy.wait_send()

    if last:
        own = out_ref.at[me]
        sends = {j: remote(fin, own, fin_send.at[j], fin_recv.at[j], peer[j]) for j in (6, 2, 4, 1)}
        for copy in sends.values():
            copy.start()
        for j in (2, 4, 6):
            sends[j].wait_recv()
            theirs = out_ref.at[peer[j]]
            sends[j + 1] = remote(theirs, theirs, fin_send.at[j + 1], fin_recv.at[j + 1], peer[1])
            sends[j + 1].start()
        for j in (1, 3, 5, 7):
            sends[j].wait_recv()
        for copy in sends.values():
            copy.wait_send()


def ffn_layer(layer, last, x_rows, gain, gain_final, w_gate, w_up, w_down):
    n_rows, d_model = x_rows.shape
    width = w_gate.shape[2]
    n_chunks = d_model // RS_CHUNK
    n_w = 2 * len(ffn_cuts(width)) + n_chunks
    vmem, any_space = pl.BlockSpec(memory_space=pltpu.VMEM), pl.BlockSpec(memory_space=pl.ANY)
    bf16, f32, dma = jnp.bfloat16, jnp.float32, pltpu.SemaphoreType.DMA
    scratch = [
        pltpu.VMEM((NUM_DEV, n_rows, d_model), bf16),
        pltpu.VMEM((d_model, width), bf16),
        pltpu.VMEM((d_model, width), bf16),
        pltpu.VMEM((width, d_model), bf16),
        pltpu.VMEM((NUM_DEV * n_rows, width), bf16),
        pltpu.VMEM((n_chunks, 4, 2, n_rows, RS_CHUNK), f32),
        pltpu.VMEM((n_chunks, 4, n_rows, RS_CHUNK), f32),
        pltpu.VMEM((n_chunks, 3, n_rows, RS_CHUNK), bf16),
        pltpu.VMEM((n_chunks, 3, n_rows, RS_CHUNK), bf16),
    ]
    if last:
        scratch.append(pltpu.VMEM((n_rows, d_model), bf16))
    scratch += [dma((n_w,)), dma((8,)), dma((8,)), dma((n_chunks,)), dma((n_chunks,)), dma((n_chunks, 3)), dma((n_chunks, 3))]
    if last:
        scratch += [dma((8,)), dma((8,))]
    out_shape = (NUM_DEV, n_rows, d_model) if last else (n_rows, d_model)
    return pl.pallas_call(
        functools.partial(ffn_kernel, layer, last),
        out_shape=jax.ShapeDtypeStruct(out_shape, bf16),
        in_specs=[vmem, vmem, vmem, any_space, any_space, any_space],
        out_specs=vmem,
        scratch_shapes=scratch,
        compiler_params=pltpu.CompilerParams(collective_id=layer, has_side_effects=True,
                                             vmem_limit_bytes=48 * 1024 * 1024),
        name=f'ffn{layer}',
    )(x_rows, gain.reshape(1, -1), gain_final.reshape(1, -1), w_gate, w_up, w_down)


def solution(mesh):
    row_axes = ('rep', 'dp')
    specs_in = (P(row_axes, None), P(row_axes), P(None, row_axes, None, None), P(), P(), P(), P(),
                P(None, None, 'dp'), P(None, None, 'dp'), P(None, 'dp', None), P(), P(None, 'dp'))

    def device_step(hidden, lengths, kv_cache, norm_attn, w_q, w_o, norm_ffn, w_gate, w_up, w_down, norm_final, w_head):
        x_rows = hidden
        num_layers = kv_cache.shape[0]
        for layer_idx in range(num_layers):
            normed = rms_norm(x_rows, norm_attn[layer_idx])
            context = mla_attention(normed, w_q[layer_idx], kv_cache[layer_idx], lengths)
            x_rows = add_residual(x_rows, jnp.dot(context, w_o[layer_idx], preferred_element_type=jnp.float32))
            x_rows = ffn_layer(layer_idx, layer_idx == num_layers - 1, x_rows, norm_ffn[layer_idx], norm_final,
                               w_gate, w_up, w_down)
        gathered = x_rows.reshape(-1, hidden.shape[1])
        return jnp.dot(gathered, w_head, preferred_element_type=jnp.float32)

    return jax.shard_map(device_step, mesh=mesh, in_specs=specs_in, out_specs=P('rep', 'dp'), check_vma=False)
```

time: 319 us -> 233 us (0.73)
  waiting for transfers between devices: 121 us -> 0 us
  Pallas kernels: 0 us -> 58.4 us
  matrix products: 151 us -> 116 us
  local copies, waits for them, and re-layouts: 27.9 us -> 57.6 us
  between operations: 13.3 us -> 0.17 us
  other arithmetic: 5.6 us -> 0.37 us
    reduce_scatter x2 -> x0, waiting for transfers between devices: 65.1 us -> none  [device_step(): ffn_out = lax.psum_scatter(part_sum, 'dp', scatter_dimension=0, tiled=True)]
    pallas_call x0 -> x2, Pallas kernels: none -> 58.4 us  [ffn_layer(): pl.pallas_call(functools.partial(ffn_kernel, layer, last), out_shape=jax....]
    all_gather x3 -> x0, waiting for transfers between devices: 55.4 us -> none  [device_step(): gathered = lax.all_gather(normed, 'dp', axis=0, tiled=True)]
    dot_general x4 -> x0, matrix products: 33.4 us -> none  [the longest x2 24.2 us: ffn_block(): return jnp.dot(act_rows, w_down, preferred_element_type=jnp.float32)]
    unnamed x10 -> x14, local copies, waits for them, and re-layouts: 0.61 us -> 31.2 us
  transfers between devices with their start and end apart: 5 -> 0, of which waited for: 5 -> 0; matrix products, arithmetic and copies ran while one was open for 0% -> 0% of each run, Pallas kernels for 0% -> 0%
where the time goes in v1:
time: 233 us; the launch traced here: 232 us
  matrix products  116 us (50%)
  Pallas kernels  58.4 us (25%)
  local copies, waits for them, and re-layouts  57.6 us (25%)
    pallas_call x2, Pallas kernels, ffn_layer(): pl.pallas_call(functools.partial(ffn_kernel, layer, last), out_shape=jax....  58.4 us
    unnamed x14, local copies, waits for them, and re-layouts  31.2 us
    dot_general x2, matrix products, mla_attention(): jnp.dot(normed, w_q, preferred_element_type=jnp.float32)  30.5 us
    dot_general x2, matrix products, device_step(): jnp.dot(context, w_o[layer_idx], preferred_element_type=jnp.float32)  27.4 us
    dot_general x1, matrix products, device_step(): return jnp.dot(gathered, w_head, preferred_element_type=jnp.float32)  25.6 us
    squeeze x1, local copies, waits for them, and re-layouts, device_step(): kv_cache[layer_idx]  25.3 us
    dot_general x2, matrix products, mla_attention(): jnp.einsum('bht,btc->bhc', attn_probs, kv_cache[:, :, :LATENT_DIM], prefe...  16.4 us
    sub x2, matrix products, mla_attention(): attn_probs = jax.nn.softmax(scores, axis=-1).astype(jnp.bfloat16)  16 us

profile of v1, /device:TPU:0, one launch (start us, length us, event | category | flops | bytes accessed | tf_op | source)
XLA Modules:
  0.0 232.4 jit_solution(3393288233875002994)
XLA Ops:
  0.0 25.3 %slice_bitcast_fusion.1 = (bf16[32,512,576]{1,2,0:T(8,128)(2,1)}, bf16[32,512,576]{1,2,0:T(8,128)(2,1)}) fusion(bf16[2,32,512,576]{2,3,1,0:T(8,128)(2,1)} %param.14), kind=kLoop, calls=%fused_computation.15 | loop fusion | bytes 75497472 | tf_op jit(solution)/shard_map/squeeze | solution.py:218
  25.4 0.1 fusion.50
  25.5 15.3 %fusion.18 = bf16[32,9216]{1,0:T(8,128)(2,1)S(1)} fusion(bf16[2,2048,9216]{2,1,0:T(8,128)(2,1)} %param.16, bf16[32,2048]{1,0:T(8,128)(2,1)S(1)} %copy-done.1, f32[2048]{0:T(1024)S(1)} %bitcast.56, f32[32]{0:T(128)S(1)} %add_rsqrt_fusion.1), kind=kOutput, calls=%fused_computation.20 | convolution fusion | flops 1208516608 | bytes 38477952 | tf_op jit(solution)/shard_map/dot_general | solution.py:26
  40.8 0.5 reshape.60
  41.3 0.0 copy-done.4
  41.3 0.1 iota_compare_fusion
  41.4 8.0 %fusion.64 = (f32[32,16]{1,0:T(8,128)S(1)}, f32[32,16,512]{2,1,0:T(8,128)S(1)}) fusion(bf16[32,16,576]{2,1,0:T(8,128)(2,1)S(1)} %reshape.60, pred[32,512]{1,0:T(8,128)(4,1)S(1)} %iota_compare_fusion, bf16[2,32,512,576]{2,3,1,0:T(8,128)(2,1)} %param.14), kind=kOutput, calls=%fused_computation.59 | convolution fusion | flops 303038976 | bytes 20531200 | tf_op jit(solution)/shard_map/sub | solution.py:31
  49.4 8.2 %fusion.42 = bf16[32,16,512]{2,1,0:T(8,128)(2,1)S(1)} fusion(bf16[32,512,576]{1,2,0:T(8,128)(2,1)} %get-tuple-element.5, f32[32,16,512]{2,1,0:T(8,128)S(1)} %get-tuple-element.12, f32[32,16]{1,0:T(8,128)S(1)} %get-tuple-element.11), kind=kOutput, calls=%fused_computation.34 | convolution fusion | flops 269221888 | bytes 18352128 | tf_op jit(solution)/shard_map/bht,btc->bhc/dot_general | solution.py:32
  57.6 0.3 copy.21
  57.9 13.6 %fusion.33.x_ref = bf16[32,2048]{1,0:T(8,128)(2,1)S(1)} fusion(bf16[32,8192]{1,0:T(8,128)(2,1)S(1)} %bitcast.54, bf16[2,8192,2048]{2,1,0:T(8,128)(2,1)} %param.17, bf16[32,2048]{1,0:T(8,128)(2,1)S(1)} %copy-done.1), kind=kOutput, calls=%fused_computation.25 | convolution fusion | flops 1073938432 | bytes 34340864 | tf_op jit(solution)/shard_map/dot_general | solution.py:219
  71.5 0.0 copy-done.3
  71.5 0.0 copy-start
  71.6 15.3 %copy.14.wg_hbm = bf16[2,2048,1368]{2,1,0:T(8,128)(2,1)} copy(bf16[2,2048,1368]{1,2,0:T(8,128)(2,1)} %param.19) | data formatting | bytes 22413312 | tf_op args[7]
  86.9 15.3 %copy.15.wu_hbm = bf16[2,2048,1368]{2,1,0:T(8,128)(2,1)} copy(bf16[2,2048,1368]{1,2,0:T(8,128)(2,1)} %param.20) | data formatting | bytes 22413312 | tf_op args[8]
  102.1 26.3 %ffn0.1 = bf16[32,2048]{1,0:T(8,128)(2,1)S(1)} custom-call(bf16[32,2048]{1,0:T(8,128)(2,1)S(1)} %fusion.33.x_ref, f32[1,2048]{1,0:T(1,128)S(1)} %get-tuple-element.8.gain_ref, f32[1,2048]{1,0:T(1,128)S(1)} %bitcast.49, bf16[2,2048,1368]{2,1,0:T(8,128)(2,1)} %copy.14.wg_hbm, bf16[2,2048,1368]{2,1,0:T(8,128)(2,1)} %copy.15.wu_hbm, bf16[2,1368,2048]{2,1,0:T(8,128)(2,1)} %wd_hbm.3), custom_call_target="tpu_custom_call" | custom-call | tf_op jit(solution)/shard_map/ffn0/pallas_call | solution.py:196
  128.4 0.1 fusion.53
  128.6 15.2 %fusion.21 = bf16[32,9216]{1,0:T(8,128)(2,1)S(1)} fusion(bf16[2,2048,9216]{2,1,0:T(8,128)(2,1)} %param.16, bf16[32,2048]{1,0:T(8,128)(2,1)S(1)} %ffn0.1, f32[2048]{0:T(1024)S(1)} %bitcast.55, f32[32]{0:T(128)S(1)} %add_rsqrt_fusion), kind=kOutput, calls=%fused_computation.21 | convolution fusion | flops 1208516608 | bytes 38477952 | tf_op jit(solution)/shard_map/dot_general | solution.py:26
  143.8 0.5 reshape.63
  144.3 8.0 %fusion.65 = (f32[32,16]{1,0:T(8,128)S(1)}, f32[32,16,512]{2,1,0:T(8,128)S(1)}) fusion(bf16[32,16,576]{2,1,0:T(8,128)(2,1)S(1)} %reshape.63, pred[32,512]{1,0:T(8,128)(4,1)S(1)} %iota_compare_fusion, bf16[2,32,512,576]{2,3,1,0:T(8,128)(2,1)} %param.14), kind=kOutput, calls=%fused_computation.60 | convolution fusion | flops 303038976 | bytes 20531200 | tf_op jit(solution)/shard_map/sub | solution.py:31
  152.3 8.2 %fusion.45 = bf16[32,16,512]{2,1,0:T(8,128)(2,1)S(1)} fusion(bf16[32,512,576]{1,2,0:T(8,128)(2,1)} %get-tuple-element.6, f32[32,16,512]{2,1,0:T(8,128)S(1)} %get-tuple-element.14, f32[32,16]{1,0:T(8,128)S(1)} %get-tuple-element.13), kind=kOutput, calls=%fused_computation.35 | convolution fusion | flops 269221888 | bytes 18352128 | tf_op jit(solution)/shard_map/bht,btc->bhc/dot_general | solution.py:32
  160.5 0.3 copy.22
  160.8 13.8 %fusion.30.x_ref = bf16[32,2048]{1,0:T(8,128)(2,1)S(1)} fusion(bf16[32,8192]{1,0:T(8,128)(2,1)S(1)} %bitcast.53, bf16[2,8192,2048]{2,1,0:T(8,128)(2,1)} %param.17, bf16[32,2048]{1,0:T(8,128)(2,1)S(1)} %ffn0.1), kind=kOutput, calls=%fused_computation.24 | convolution fusion | flops 1073938432 | bytes 34340864 | tf_op jit(solution)/shard_map/dot_general | solution.py:219
  174.6 32.2 %ffn1.1 = bf16[8,32,2048]{2,1,0:T(8,128)(2,1)S(1)} custom-call(bf16[32,2048]{1,0:T(8,128)(2,1)S(1)} %fusion.30.x_ref, f32[1,2048]{1,0:T(1,128)S(1)} %get-tuple-element.7.gain_ref, f32[1,2048]{1,0:T(1,128)S(1)} %bitcast.50, bf16[2,2048,1368]{2,1,0:T(8,128)(2,1)} %copy.14.wg_hbm, bf16[2,2048,1368]{2,1,0:T(8,128)(2,1)} %copy.15.wu_hbm, ...), custom_call_target="tpu_custom_call" | custom-call | tf_op jit(solution)/shard_map/ffn1/pallas_call | solution.py:196
  206.8 25.6 %fusion.66 = f32[256,12800]{1,0:T(8,128)} fusion(bf16[256,2048]{1,0:T(8,128)(2,1)S(1)} %bitcast.48, bf16[2048,12800]{1,0:T(8,128)(2,1)} %param.23), kind=kOutput, calls=%fused_computation.61 | convolution fusion | flops 13421772800 | bytes 66584576 | tf_op jit(solution)/shard_map/dot_general | solution.py:223
  (11 shorter events, 0.1 us)
Async XLA Ops:
  0.0 25.3 %copy-start.1 = (bf16[32,2048]{1,0:T(8,128)(2,1)S(1)}, bf16[32,2048]{1,0:T(8,128)(2,1)}, u32[]{:S(2)}) copy-start(bf16[32,2048]{1,0:T(8,128)(2,1)} %param.12) | copy-start | bytes 393220
  0.0 25.3 %copy-start.2 = (f32[2,2048]{1,0:T(2,128)S(1)}, f32[2,2048]{1,0:T(2,128)}, u32[]{:S(2)}) copy-start(f32[2,2048]{1,0:T(2,128)} %param.15) | copy-start | bytes 49156
  25.3 16.0 %copy-start.4 = (s32[32]{0:T(128)S(1)}, s32[32]{0:T(128)}, u32[]{:S(2)}) copy-start(s32[32]{0:T(128)} %param.13) | copy-start | bytes 388
  49.4 22.1 %copy-start.3 = (f32[2,2048]{1,0:T(2,128)S(1)}, f32[2,2048]{1,0:T(2,128)}, u32[]{:S(2)}) copy-start(f32[2,2048]{1,0:T(2,128)} %param.18) | copy-start | bytes 49156
  71.5 30.6 %copy-start = (f32[2048]{0:T(1024)S(1)}, f32[2048]{0:T(1024)}, u32[]{:S(2)}) copy-start(f32[2048]{0:T(1024)} %param.22) | copy-start | bytes 24580

commit v2 on v0

v2 whole, which is shorter than its diff:
```python
import functools

import jax
import jax.numpy as jnp
from jax import lax
from jax.experimental import pallas as pl
from jax.experimental.pallas import tpu as pltpu
from jax.sharding import PartitionSpec as P

LATENT = 512
QK_SCALE = 192 ** -0.5
NORM_EPS = 1e-6
MESH_ID = pl.DeviceIdType.MESH
NUM_DEV = 8
CHUNK = 512
GROUP = 4
BF16, F32 = jnp.bfloat16, jnp.float32


def rms_norm(x_rows, gain_vec):
    x_float = x_rows.astype(F32)
    inv_rms = lax.rsqrt(jnp.mean(x_float * x_float, axis=-1, keepdims=True) + NORM_EPS)
    return (x_float * inv_rms * gain_vec).astype(BF16)


def dot(a, b):
    return jnp.dot(a, b, preferred_element_type=F32)


def dot_nt(a, b):
    return lax.dot_general(a, b, (((1,), (1,)), ((), ())), preferred_element_type=F32)


def round_up(n, m):
    return (n + m - 1) // m * m


def cuts_of(width):
    return [(lo, min(lo + CHUNK, width)) for lo in range(0, width, CHUNK)]


def layers_kernel(dims, x_ref, len_ref, gain_attn, gain_ffn, gain_fin, kv_hbm, wq_hbm, wo_hbm, wg_hbm, wu_hbm, wd_hbm,
                  rows, buf, x_cur, hrows, qo, qsend, p_buf, ol, ol_send, ps, pr, act, pair_send, pair_in, total, chip_in,
                  fin, wq_sem, kv_sem, wo_sem, ffn_sem, h_sem, q_sem, o_sem, p_sem, ag_sem, pair_sem, chip_sem, fin_sem):
    n_layers, n_rows, d_model, n_heads, kv_width, seq_len, width, pad_width = dims
    half = n_heads // 2
    q_cols = half * kv_width
    n_q, n_d = q_cols // CHUNK, d_model // CHUNK
    o_rows = half * LATENT
    n_t = round_up(kv_width, 128) // 128
    cuts = cuts_of(width)

    me = lax.axis_index('dp')
    core, x_pos, y_pos = me % 2, (me // 2) % 2, me // 4
    flip = lambda c, a, b: ((y_pos + b) % 2) * 4 + ((x_pos + a) % 2) * 2 + (core + c) % 2
    peer = {1: flip(1, 0, 0), 2: flip(0, 1, 0), 4: flip(0, 0, 1), 6: flip(0, 1, 1)}
    other = 1 - core

    def remote(src, dst, sems, dev):
        return pltpu.make_async_remote_copy(src_ref=src, dst_ref=dst, send_sem=sems.at[0], recv_sem=sems.at[1],
                                            device_id={'dp': dev}, device_id_type=MESH_ID)

    wq_buf = lambda l: l % 3
    kv_buf = lambda l: (l + 1) % 3
    wo_buf = lambda l: (l + 2) % 3
    ffn_buf = wq_buf

    def wq_copy(l, n):
        cols = pl.ds(pl.multiple_of(core * q_cols + n * CHUNK, 128), CHUNK)
        return pltpu.make_async_copy(wq_hbm.at[l, :, cols], buf.at[wq_buf(l), pl.ds(n * d_model, d_model)], wq_sem.at[l, n])

    def kv_copy(l, b):
        row = b * kv_width if isinstance(b, int) else pl.multiple_of(b * kv_width, 64)
        return pltpu.make_async_copy(kv_hbm.at[l, b], buf.at[kv_buf(l), pl.ds(row, kv_width)], kv_sem.at[l, b])

    def wo_copy(l, n):
        src = wo_hbm.at[l, pl.ds(pl.multiple_of(core * o_rows, 128), o_rows), pl.ds(n * CHUNK, CHUNK)]
        return pltpu.make_async_copy(src, buf.at[wo_buf(l), pl.ds(n * o_rows, o_rows)], wo_sem.at[l, n])

    def ffn_copy(l, i):
        src = (wg_hbm, wu_hbm, wd_hbm)[i // n_d]
        return pltpu.make_async_copy(src.at[l, :, pl.ds((i % n_d) * CHUNK, CHUNK)],
                                     buf.at[ffn_buf(l), pl.ds(i * pad_width, width)], ffn_sem.at[l, i])

    def start(copies):
        for copy in copies:
            copy.start()

    def gather(own, slot_of, sems):
        sends = {j: remote(own, slot_of(0, j), sems.at[j], peer[j]) for j in (6, 2, 4, 1)}
        start(sends.values())
        for j in (2, 4, 6):
            sends[j].wait_recv()
            sends[j + 1] = remote(slot_of(j, j), slot_of(j, j + 1), sems.at[j + 1], peer[1])
            sends[j + 1].start()
        for j in (1, 3, 5, 7):
            sends[j].wait_recv()
        return list(sends.values())

    start(wq_copy(0, n) for n in range(n_q))
    x_cur[...] = x_ref[...]

    for l in range(n_layers):
        sent = []
        hrows[0] = rms_norm(x_cur[...], gain_attn[pl.ds(l, 1), :])
        if l == 0:
            barrier = pltpu.get_barrier_semaphore()
            for j in (1, 2, 4, 6):
                pl.semaphore_signal(barrier, inc=1, device_id={'dp': peer[j]}, device_id_type=MESH_ID)
            pl.semaphore_wait(barrier, 4)
        copy = remote(hrows.at[0], hrows.at[1], h_sem.at[l], peer[1])
        copy.start()
        sent.append(copy)
        copy.wait_recv()
        both_rows = hrows[...].reshape(2 * n_rows, d_model)
        prev, q_copies = None, []
        for n in range(n_q):
            wq_copy(l, n).wait()
            if l == 0:
                per = -(-n_rows // n_q)
                start(kv_copy(l, b) for b in range(n * per, min((n + 1) * per, n_rows)))
            cur = dot(both_rows, buf[wq_buf(l), pl.ds(n * d_model, d_model), :]).astype(BF16).astype(F32)
            if n >= 1:
                h = n - 1
                off = h * kv_width - h * CHUNK
                q_head = jnp.concatenate([prev[:, off:], cur[:, :off + kv_width - CHUNK]], axis=1)
                for j in range(n_t):
                    lanes = slice(j * 128, min((j + 1) * 128, kv_width))
                    keep = pl.ds(0, lanes.stop - lanes.start)
                    qo[j, pl.ds(pl.multiple_of((core * half + h) * n_rows, n_rows), n_rows), keep] = q_head[:n_rows, lanes]
                    qsend[j, pl.ds(h * n_rows, n_rows), keep] = q_head[n_rows:, lanes]
                if h % 2:
                    dst = qo.at[:, pl.ds(pl.multiple_of((core * half + h - 1) * n_rows, n_rows), 2 * n_rows)]
                    copy = remote(qsend.at[:, pl.ds((h - 1) * n_rows, 2 * n_rows)], dst, q_sem.at[l, h // 2], peer[1])
                    copy.start()
                    q_copies.append(copy)
            prev = cur
        if l == 0:
            start(wo_copy(l, n) for n in range(n_d))
        sent += q_copies
        for copy in q_copies:
            copy.wait_recv()

        key_pos = lax.broadcasted_iota(jnp.int32, (n_heads, seq_len), 1)

        def scores(g, l=l):
            slot = lax.rem(g, 2)
            for i in range(GROUP):
                b = g * GROUP + i
                kv_copy(l, b).wait()
                q = [qo[j, pl.ds(b, n_heads, stride=n_rows), :].astype(BF16) for j in range(n_t)]
                q = jnp.concatenate(q, axis=1)[:, :kv_width]
                row = pl.multiple_of(b * kv_width, 64)
                s = dot(q, buf[kv_buf(l), pl.ds(row, kv_width), :]) * QK_SCALE
                s = jnp.where(key_pos < len_ref[b], s, -1e30)
                e = jnp.exp(s - jnp.max(s, axis=-1, keepdims=True))
                p_buf[slot, i] = (e / jnp.sum(e, axis=-1, keepdims=True)).astype(BF16)

        def contexts(g, l=l):
            slot = lax.rem(g, 2)
            for i in range(GROUP):
                b = g * GROUP + i
                row = pl.multiple_of(b * kv_width, 64)
                ctx = dot_nt(p_buf[slot, i], buf[kv_buf(l), pl.ds(row, LATENT), :])
                for j in range(LATENT // 128):
                    qo[j, pl.ds(b, n_heads, stride=n_rows), :] = ctx[:, j * 128:(j + 1) * 128]

        n_groups = n_rows // GROUP
        scores(jnp.int32(0))

        def step(g, carry):
            scores(g)
            contexts(g - 1)
            return carry

        lax.fori_loop(1, n_groups, step, 0)
        contexts(jnp.int32(n_groups - 1))

        for h in range(half):
            at = pl.ds(pl.multiple_of((other * half + h) * n_rows, n_rows), n_rows)
            for j in range(LATENT // 128):
                ol_send[h, :, pl.ds(j * 128, 128)] = qo[j, at, :].astype(BF16)
        o_copy = remote(ol_send, ol.at[1], o_sem.at[l], peer[1])
        o_copy.start()
        sent.append(o_copy)
        start(ffn_copy(l, i) for i in range(3 * n_d))
        for h in range(half):
            at = pl.ds(pl.multiple_of((core * half + h) * n_rows, n_rows), n_rows)
            for j in range(LATENT // 128):
                ol[0, h, :, pl.ds(j * 128, 128)] = qo[j, at, :].astype(BF16)
        o_copy.wait_recv()
        p_copies, own = [], []
        for n in range(n_d):
            wo_copy(l, n).wait()
            acc = None
            for h in range(half):
                part = dot(ol[:, h].reshape(2 * n_rows, LATENT), buf[wo_buf(l), pl.ds(n * o_rows + h * LATENT, LATENT), :])
                acc = part if acc is None else acc + part
            own.append(acc[:n_rows])
            ps[n] = acc[n_rows:]
            copy = remote(ps.at[n], pr.at[n], p_sem.at[l, n], peer[1])
            copy.start()
            p_copies.append(copy)
        sent += p_copies
        for n in range(n_d):
            cols = pl.ds(n * CHUNK, CHUNK)
            p_copies[n].wait_recv()
            x_cur[:, cols] = (x_cur[:, cols].astype(F32) + (own[n] + pr[n])).astype(BF16)

        rows[0] = rms_norm(x_cur[...], gain_ffn[pl.ds(l, 1), :])
        row_sends = gather(rows.at[0], lambda j, k: rows.at[k], ag_sem.at[l])
        if l + 1 < n_layers:
            start(wq_copy(l + 1, n) for n in range(n_q))
        for i in range(2 * n_d):
            ffn_copy(l, i).wait()
        for lo, hi in cuts:
            gate = up = None
            for k in range(n_d):
                cols = rows[:, :, pl.ds(k * CHUNK, CHUNK)].reshape(NUM_DEV * n_rows, CHUNK)
                g_part = dot_nt(cols, buf[ffn_buf(l), pl.ds(k * pad_width + lo, hi - lo), :])
                u_part = dot_nt(cols, buf[ffn_buf(l), pl.ds((n_d + k) * pad_width + lo, hi - lo), :])
                gate = g_part if gate is None else gate + g_part
                up = u_part if up is None else up + u_part
            act[:, pl.ds(lo, hi - lo)] = (jax.nn.silu(gate) * up).astype(BF16)

        for copy in row_sends:
            copy.wait_send()
        pair, chip = [], []

        def reduce_chunk(c):
            pair[c].wait_recv()
            for k in range(4):
                at = pl.ds((c * 4 + k) * n_rows, n_rows)
                for j in range(CHUNK // 128):
                    lanes = pl.ds(j * 128, 128)
                    both = qo[j, at, :] + pair_in[c, k, :, lanes]
                    if k == 0:
                        qo[j, at, :] = both
                    else:
                        total[c, k - 1, :, lanes] = both.astype(BF16)
            for k in (3, 1, 2):
                copy = remote(total.at[c, k - 1], chip_in.at[c, k - 1], chip_sem.at[l, c, k - 1], peer[2 * k])
                copy.start()
                chip.append(copy)

        for c in range(n_d):
            ffn_copy(l, 2 * n_d + c).wait()
            y = dot(act[...], buf[ffn_buf(l), pl.ds((2 * n_d + c) * pad_width, width), :])
            y = y.reshape(4, 2, n_rows, CHUNK)
            pair_send[c] = y[:, 1]
            mine = y[:, 0].reshape(4 * n_rows, CHUNK)
            for j in range(CHUNK // 128):
                qo[j, pl.ds(c * 4 * n_rows, 4 * n_rows), :] = mine[:, j * 128:(j + 1) * 128]
            copy = remote(pair_send.at[c], pair_in.at[c], pair_sem.at[l, c], peer[1])
            copy.start()
            pair.append(copy)
            if c >= 1:
                reduce_chunk(c - 1)
        reduce_chunk(n_d - 1)
        if l + 1 < n_layers:
            start(kv_copy(l + 1, b) for b in range(n_rows))
            start(wo_copy(l + 1, n) for n in range(n_d))
        for copy in chip:
            copy.wait_recv()
        for c in range(n_d):
            cols = pl.ds(c * CHUNK, CHUNK)
            y = jnp.concatenate([qo[j, pl.ds(c * 4 * n_rows, n_rows), :] for j in range(CHUNK // 128)], axis=1)
            for k in range(3):
                y = y + chip_in[c, k].astype(F32)
            x_cur[:, cols] = (x_cur[:, cols].astype(F32) + y).astype(BF16)
        for copy in sent + pair + chip:
            copy.wait_send()

    fin[...] = rms_norm(x_cur[...], gain_fin[...])
    rows[me] = fin[...]
    peer[0] = me
    sends = gather(fin, lambda j, k: rows.at[peer[j]], fin_sem)
    for copy in sends:
        copy.wait_send()


def run_layers(hidden, lengths, kv_t, gain_attn, w_q, w_o, gain_ffn, wg_t, wu_t, w_down, gain_fin):
    n_layers, n_rows, kv_width, seq_len = kv_t.shape
    d_model = hidden.shape[1]
    n_heads = w_q.shape[2] // kv_width
    width = w_down.shape[1]
    pad_width = round_up(width, 16)
    half, n_d = n_heads // 2, d_model // CHUNK
    n_q = half * kv_width // CHUNK
    n_t = round_up(kv_width, 128) // 128
    buf_rows = max(n_q * d_model, n_rows * kv_width, n_d * half * LATENT, 3 * n_d * pad_width)
    dims = (n_layers, n_rows, d_model, n_heads, kv_width, seq_len, width, pad_width)
    vmem, anys = pl.BlockSpec(memory_space=pltpu.VMEM), pl.BlockSpec(memory_space=pl.ANY)
    smem = pl.BlockSpec(memory_space=pltpu.SMEM)
    dma = pltpu.SemaphoreType.DMA
    scratch = [
        pltpu.VMEM((3, buf_rows, CHUNK), BF16),
        pltpu.VMEM((n_rows, d_model), BF16),
        pltpu.VMEM((2, n_rows, d_model), BF16),
        pltpu.VMEM((n_t, n_heads * n_rows, 128), F32),
        pltpu.VMEM((n_t, half * n_rows, 128), F32),
        pltpu.VMEM((2, GROUP, n_heads, seq_len), BF16),
        pltpu.VMEM((2, half, n_rows, LATENT), BF16),
        pltpu.VMEM((half, n_rows, LATENT), BF16),
        pltpu.VMEM((n_d, n_rows, CHUNK), F32),
        pltpu.VMEM((n_d, n_rows, CHUNK), F32),
        pltpu.VMEM((NUM_DEV * n_rows, width), BF16),
        pltpu.VMEM((n_d, 4, n_rows, CHUNK), F32),
        pltpu.VMEM((n_d, 4, n_rows, CHUNK), F32),
        pltpu.VMEM((n_d, 3, n_rows, CHUNK), BF16),
        pltpu.VMEM((n_d, 3, n_rows, CHUNK), BF16),
        pltpu.VMEM((n_rows, d_model), BF16),
        dma((n_layers, n_q)), dma((n_layers, n_rows)), dma((n_layers, n_d)), dma((n_layers, 3 * n_d)),
        dma((n_layers, 2)), dma((n_layers, half // 2, 2)), dma((n_layers, 2)), dma((n_layers, n_d, 2)),
        dma((n_layers, 8, 2)), dma((n_layers, n_d, 2)), dma((n_layers, n_d, 3, 2)), dma((8, 2)),
    ]
    return pl.pallas_call(
        functools.partial(layers_kernel, dims),
        out_shape=jax.ShapeDtypeStruct((NUM_DEV, n_rows, d_model), BF16),
        in_specs=[vmem, smem, vmem, vmem, vmem] + [anys] * 6,
        out_specs=vmem,
        scratch_shapes=scratch,
        compiler_params=pltpu.CompilerParams(collective_id=0, has_side_effects=True, vmem_limit_bytes=67043328),
        name='layers',
    )(hidden, lengths, gain_attn, gain_ffn, gain_fin.reshape(1, -1), kv_t, w_q, w_o, wg_t, wu_t, w_down)


def solution(mesh):
    row_axes = ('rep', 'dp')
    specs_in = (P(row_axes, None), P(row_axes), P(None, row_axes, None, None), P(), P(), P(), P(),
                P(None, None, 'dp'), P(None, None, 'dp'), P(None, 'dp', None), P(), P(None, 'dp'))

    def device_step(hidden, lengths, kv_cache, norm_attn, w_q, w_o, norm_ffn, w_gate, w_up, w_down, norm_final, w_head):
        gathered = run_layers(hidden, lengths, jnp.swapaxes(kv_cache, 2, 3), norm_attn, w_q, w_o, norm_ffn,
                              jnp.swapaxes(w_gate, 1, 2), jnp.swapaxes(w_up, 1, 2), w_down, norm_final)
        return dot(gathered.reshape(-1, hidden.shape[1]), w_head)

    return jax.shard_map(device_step, mesh=mesh, in_specs=specs_in, out_specs=P('rep', 'dp'), check_vma=False)
```

time: 319 us -> 145 us (0.45)
  matrix products: 151 us -> 27.2 us
  waiting for transfers between devices: 121 us -> 0 us
  Pallas kernels: 0 us -> 118 us
  local copies, waits for them, and re-layouts: 27.9 us -> 0 us
  between operations: 13.3 us -> 0.01 us
  other arithmetic: 5.6 us -> 0 us
    pallas_call x0 -> x1, Pallas kernels: none -> 118 us  [run_layers(): pl.pallas_call(functools.partial(layers_kernel, dims), out_shape=jax.Shap...]
    dot_general x11 -> x1, matrix products: 135 us -> 27.2 us  [dot(): return jnp.dot(a, b, preferred_element_type=F32)]
    reduce_scatter x2 -> x0, waiting for transfers between devices: 65.1 us -> none  [device_step(): ffn_out = lax.psum_scatter(part_sum, 'dp', scatter_dimension=0, tiled=True)]
    all_gather x3 -> x0, waiting for transfers between devices: 55.4 us -> none  [device_step(): gathered = lax.all_gather(normed, 'dp', axis=0, tiled=True)]
    squeeze x1 -> x0, local copies, waits for them, and re-layouts: 25.4 us -> none  [device_step(): kv_cache[layer_idx]]
    sub x2 -> x0, matrix products: 16 us -> none  [mla_attention(): attn_probs = jax.nn.softmax(scores, axis=-1).astype(jnp.bfloat16)]
    reduce_sum x3 -> x0, other arithmetic: 3.22 us -> none  [rms_norm(): jnp.mean(x_float * x_float, axis=-1, keepdims=True) + NORM_EPS]
  transfers between devices with their start and end apart: 5 -> 0, of which waited for: 5 -> 0; matrix products, arithmetic and copies ran while one was open for 0% -> 0% of each run, Pallas kernels for 0% -> 0%
where the time goes in v2:
time: 145 us
  Pallas kernels  118 us (81%)
  matrix products  27.2 us (19%)
    pallas_call x1, Pallas kernels, run_layers(): pl.pallas_call(functools.partial(layers_kernel, dims), out_shape=jax.Shap...  118 us
    dot_general x1, matrix products, dot(): return jnp.dot(a, b, preferred_element_type=F32)  27.2 us

profile of v2, /device:TPU:0, one launch (start us, length us, event | category | flops | bytes accessed | tf_op | source)
XLA Modules:
  0.0 144.9 jit_solution(10572233606478832665)
XLA Ops:
  0.0 117.7 %layers.1 = bf16[8,32,2048]{2,1,0:T(8,128)(2,1)} custom-call(bf16[32,2048]{1,0:T(8,128)(2,1)} %x_ref.1, s32[32]{0:T(128)} %len_ref.1, f32[2,2048]{1,0:T(2,128)} %gain_attn.1, f32[2,2048]{1,0:T(2,128)} %gain_ffn.1, f32[1,2048]{1,0:T(1,128)} %bitcast.11, bf16[2,32,576,512]{3,2,1,0:T(8,128)(2,1)} %bitcast.7, bf16[2,2048,9216]{2,1,0:T(8,128)(2,1)} %wq_hbm.1, ...), custom_call_target="tpu_custom_call" | custom-call | tf_op jit(solution)/shard_map/layers/pallas_call | solution.py:317
  117.7 27.2 %fusion = f32[256,12800]{1,0:T(8,128)} fusion(bf16[256,2048]{1,0:T(8,128)(2,1)} %bitcast.10, bf16[2048,12800]{1,0:T(8,128)(2,1)} %param.23), kind=kOutput, calls=%fused_computation | convolution fusion | flops 13421772800 | bytes 66584576 | tf_op jit(solution)/shard_map/dot_general | solution.py:27

commit v3 on v2

v3 whole, which is shorter than its diff:
```python
import functools

import jax
import jax.numpy as jnp
from jax import lax
from jax.experimental import pallas as pl
from jax.experimental.pallas import tpu as pltpu
from jax.sharding import PartitionSpec as P

LATENT = 512
QK_SCALE = 192 ** -0.5
NORM_EPS = 1e-6
MESH_ID = pl.DeviceIdType.MESH
NUM_DEV = 8
CHUNK = 512
GROUP = 8
HEAD_A, HEAD_B = 16, 9
VMEM_LAYERS = int(8.9 * 2**20)
BF16, F32 = jnp.bfloat16, jnp.float32


def rms_norm(x_rows, gain_vec):
    x_float = x_rows.astype(F32)
    inv_rms = lax.rsqrt(jnp.mean(x_float * x_float, axis=-1, keepdims=True) + NORM_EPS)
    return (x_float * inv_rms * gain_vec).astype(BF16)


def dot(a, b):
    return jnp.dot(a, b, preferred_element_type=F32)


def dot_nt(a, b):
    return lax.dot_general(a, b, (((1,), (1,)), ((), ())), preferred_element_type=F32)


def round_up(n, m):
    return (n + m - 1) // m * m


def head_chunk(i):
    return i + i // HEAD_A * 2


def cuts_of(width):
    return [(lo, min(lo + CHUNK, width)) for lo in range(0, width, CHUNK)]


def layers_kernel(dims, x_ref, len_ref, gain_attn, gain_ffn, gain_fin, kv_hbm, wq_hbm, wo_hbm, wg_hbm, wu_hbm, wd_hbm,
                  wh_hbm, rows, buf, x_cur, hrows, qo, outbox, p_buf, ol, ol_send, pr, act, pair_in, total, chip_in,
                  wq_sem, kv_sem, wo_sem, ffn_sem, h_sem, q_sem, o_sem, p_sem, ag_sem, pair_sem, chip_sem, fin_sem, head_sem):
    n_layers, n_rows, d_model, n_heads, kv_width, seq_len, width, pad_width, slot_rows, vocab = dims
    half = n_heads // 2
    q_cols = half * kv_width
    n_q, n_d = q_cols // CHUNK, d_model // CHUNK
    o_rows = half * LATENT
    n_t, n_j = round_up(kv_width, 128) // 128, CHUNK // 128
    cuts = cuts_of(width)
    n_vocab = vocab // CHUNK

    me = lax.axis_index('dp')
    core, x_pos, y_pos = me % 2, (me // 2) % 2, me // 4
    flip = lambda c, a, b: ((y_pos + b) % 2) * 4 + ((x_pos + a) % 2) * 2 + (core + c) % 2
    peer = {1: flip(1, 0, 0), 2: flip(0, 1, 0), 4: flip(0, 0, 1), 6: flip(0, 1, 1)}
    other = 1 - core

    def remote(src, dst, sems, dev):
        return pltpu.make_async_remote_copy(src_ref=src, dst_ref=dst, send_sem=sems.at[0], recv_sem=sems.at[1],
                                            device_id={'dp': dev}, device_id_type=MESH_ID)

    wq_at = lambda l, row, n: pl.ds(l % 3 * slot_rows + row, n)
    kv_at = lambda l, row, n: pl.ds((l + 1) % 3 * slot_rows + row, n)
    wo_at = lambda l, row, n: pl.ds((l + 2) % 3 * slot_rows + row, n)
    ffn_at = wq_at

    def wq_copy(l, n):
        cols = pl.ds(pl.multiple_of(core * q_cols + n * CHUNK, 128), CHUNK)
        return pltpu.make_async_copy(wq_hbm.at[l, :, cols], buf.at[wq_at(l, n * d_model, d_model)], wq_sem.at[l, n])

    def kv_copy(l, b):
        row = b * kv_width if isinstance(b, int) else pl.multiple_of(b * kv_width, 64)
        return pltpu.make_async_copy(kv_hbm.at[l, b], buf.at[kv_at(l, row, kv_width)], kv_sem.at[l, b])

    def wo_copy(l, n):
        src = wo_hbm.at[l, pl.ds(pl.multiple_of(core * o_rows, 128), o_rows), pl.ds(n * CHUNK, CHUNK)]
        return pltpu.make_async_copy(src, buf.at[wo_at(l, n * o_rows, o_rows)], wo_sem.at[l, n])

    def ffn_copy(l, i):
        src = (wg_hbm, wu_hbm, wd_hbm)[i // n_d]
        return pltpu.make_async_copy(src.at[l, :, pl.ds((i % n_d) * CHUNK, CHUNK)],
                                     buf.at[ffn_at(l, i * pad_width, width)], ffn_sem.at[l, i])

    def head_copy(i):
        row = head_chunk(i) * d_model
        return pltpu.make_async_copy(wh_hbm.at[:, pl.ds(i * CHUNK, CHUNK)], buf.at[pl.ds(row, d_model)], head_sem.at[i])

    def start(copies):
        for copy in copies:
            copy.start()

    def gather(own, slot_of, sems):
        sends = {j: remote(own, slot_of(0, j), sems.at[j], peer[j]) for j in (6, 2, 4, 1)}
        start(sends.values())
        for j in (2, 4, 6):
            sends[j].wait_recv()
            sends[j + 1] = remote(slot_of(j, j), slot_of(j, j + 1), sems.at[j + 1], peer[1])
            sends[j + 1].start()
        for j in (1, 3, 5, 7):
            sends[j].wait_recv()
        return list(sends.values())

    start(wq_copy(0, n) for n in range(n_q))
    x_cur[...] = x_ref[...]

    for l in range(n_layers):
        sent = []
        hrows[0] = rms_norm(x_cur[...], gain_attn[pl.ds(l, 1), :])
        if l == 0:
            barrier = pltpu.get_barrier_semaphore()
            for j in (1, 2, 4, 6):
                pl.semaphore_signal(barrier, inc=1, device_id={'dp': peer[j]}, device_id_type=MESH_ID)
            pl.semaphore_wait(barrier, 4)
        copy = remote(hrows.at[0], hrows.at[1], h_sem.at[l], peer[1])
        copy.start()
        sent.append(copy)
        copy.wait_recv()
        both_rows = hrows[...].reshape(2 * n_rows, d_model)
        prev, q_copies = None, []
        for first in range(0, n_q, 3):
            for n in range(first, first + 3):
                wq_copy(l, n).wait()
            if l == 0:
                per = -(-3 * n_rows // n_q)
                start(kv_copy(l, b) for b in range(first // 3 * per, min((first // 3 + 1) * per, n_rows)))
            weights = jnp.concatenate([buf[wq_at(l, n * d_model, d_model), :] for n in range(first, first + 3)], axis=1)
            wide = dot(both_rows, weights).astype(BF16).astype(F32)
            for n in range(first, first + 3):
                cur = wide[:, (n - first) * CHUNK:(n - first + 1) * CHUNK]
                if n >= 1:
                    h = n - 1
                    off = h * kv_width - h * CHUNK
                    q_head = jnp.concatenate([prev[:, off:], cur[:, :off + kv_width - CHUNK]], axis=1)
                    for j in range(n_t):
                        lanes = slice(j * 128, min((j + 1) * 128, kv_width))
                        keep = pl.ds(0, lanes.stop - lanes.start)
                        at = pl.ds(pl.multiple_of((core * half + h) * n_rows, n_rows), n_rows)
                        qo[j, at, keep] = q_head[:n_rows, lanes]
                        outbox[j, pl.ds(h * n_rows, n_rows), keep] = q_head[n_rows:, lanes]
                    if h % 2:
                        dst = qo.at[:, pl.ds(pl.multiple_of((core * half + h - 1) * n_rows, n_rows), 2 * n_rows)]
                        copy = remote(outbox.at[pl.ds(0, n_t), pl.ds((h - 1) * n_rows, 2 * n_rows)], dst, q_sem.at[l, h // 2], peer[1])
                        copy.start()
                        q_copies.append(copy)
                prev = cur
        if l == 0:
            start(wo_copy(l, n) for n in range(n_d))
        for copy in q_copies:
            copy.wait_recv()

        key_pos = lax.broadcasted_iota(jnp.int32, (n_heads, seq_len), 1)

        def scores(g, l=l):
            slot = lax.rem(g, 2)
            for i in range(GROUP):
                kv_copy(l, g * GROUP + i).wait()
            for i in range(GROUP):
                b = g * GROUP + i
                q = [qo[j, pl.ds(b, n_heads, stride=n_rows), :].astype(BF16) for j in range(n_t)]
                q = jnp.concatenate(q, axis=1)[:, :kv_width]
                row = pl.multiple_of(b * kv_width, 64)
                s = dot(q, buf[kv_at(l, row, kv_width), :]) * QK_SCALE
                s = jnp.where(key_pos < len_ref[b], s, -1e30)
                e = jnp.exp(s - jnp.max(s, axis=-1, keepdims=True))
                p_buf[slot, i] = (e / jnp.sum(e, axis=-1, keepdims=True)).astype(BF16)

        def contexts(g, l=l):
            slot = lax.rem(g, 2)
            for i in range(GROUP):
                b = g * GROUP + i
                row = pl.multiple_of(b * kv_width, 64)
                ctx = dot_nt(p_buf[slot, i], buf[kv_at(l, row, LATENT), :])
                for j in range(n_j):
                    qo[j, pl.ds(b, n_heads, stride=n_rows), :] = ctx[:, j * 128:(j + 1) * 128]

        n_groups = n_rows // GROUP
        scores(jnp.int32(0))

        def step(g, carry):
            scores(g)
            contexts(g - 1)
            return carry

        lax.fori_loop(1, n_groups, step, 0)
        contexts(jnp.int32(n_groups - 1))
        if l + 1 == n_layers:
            start(head_copy(i) for i in range(HEAD_A, n_vocab))

        for copy in q_copies:
            copy.wait_send()

        for h in range(half):
            at = pl.ds(pl.multiple_of((other * half + h) * n_rows, n_rows), n_rows)
            for j in range(n_j):
                ol_send[h, :, pl.ds(j * 128, 128)] = qo[j, at, :].astype(BF16)
        o_copy = remote(ol_send, ol.at[1], o_sem.at[l], peer[1])
        o_copy.start()
        sent.append(o_copy)
        start(ffn_copy(l, i) for i in range(3 * n_d))
        for h in range(half):
            at = pl.ds(pl.multiple_of((core * half + h) * n_rows, n_rows), n_rows)
            for j in range(n_j):
                ol[0, h, :, pl.ds(j * 128, 128)] = qo[j, at, :].astype(BF16)
        o_copy.wait_recv()
        p_copies, own = [], []
        context = jnp.concatenate([ol[:, h].reshape(2 * n_rows, LATENT) for h in range(half)], axis=1)
        for first in range(0, n_d, 2):
            for n in (first, first + 1):
                wo_copy(l, n).wait()
            weights = jnp.concatenate([buf[wo_at(l, n * o_rows, o_rows), :] for n in (first, first + 1)], axis=1)
            acc = dot(context, weights)
            for n in (first, first + 1):
                cols = slice((n - first) * CHUNK, (n - first + 1) * CHUNK)
                own.append(acc[:n_rows, cols])
                for j in range(n_j):
                    outbox[n, pl.ds(j * n_rows, n_rows), :] = acc[n_rows:, cols][:, j * 128:(j + 1) * 128]
                copy = remote(outbox.at[n, pl.ds(0, n_j * n_rows)], pr.at[n], p_sem.at[l, n], peer[1])
                copy.start()
                p_copies.append(copy)
        if l + 1 == n_layers:
            start(head_copy(i) for i in range(HEAD_B))
        for n in range(n_d):
            cols = pl.ds(n * CHUNK, CHUNK)
            p_copies[n].wait_recv()
            theirs = jnp.concatenate([pr[n, pl.ds(j * n_rows, n_rows), :] for j in range(n_j)], axis=1)
            x_cur[:, cols] = (x_cur[:, cols].astype(F32) + (own[n] + theirs)).astype(BF16)

        rows[0] = rms_norm(x_cur[...], gain_ffn[pl.ds(l, 1), :])
        row_sends = gather(rows.at[0], lambda j, k: rows.at[k], ag_sem.at[l])
        if l + 1 < n_layers:
            start(wq_copy(l + 1, n) for n in range(n_q))
        for i in range(2 * n_d):
            ffn_copy(l, i).wait()
        all_rows = rows[...].reshape(NUM_DEV * n_rows, d_model)
        for lo, hi in cuts:
            w_part = [jnp.concatenate([buf[ffn_at(l, (u * n_d + k) * pad_width + lo, hi - lo), :] for k in range(n_d)], axis=1)
                      for u in (0, 1)]
            gate = dot_nt(all_rows, w_part[0])
            up = dot_nt(all_rows, w_part[1])
            act[:, pl.ds(lo, hi - lo)] = (jax.nn.silu(gate) * up).astype(BF16)

        for copy in row_sends + p_copies:
            copy.wait_send()
        pair, chip = [], []

        def reduce_chunk(c):
            pair[c].wait_recv()
            for k in range(4):
                at = pl.ds((c * 4 + k) * n_rows, n_rows)
                for j in range(n_j):
                    lanes = pl.ds(j * 128, 128)
                    both = qo[j, at, :] + pair_in[2 * c + j // 2, pl.ds((j % 2 * 4 + k) * n_rows, n_rows), :]
                    if k == 0:
                        qo[j, at, :] = both
                    else:
                        total[c, k - 1, :, lanes] = both.astype(BF16)
            for k in (3, 1, 2):
                copy = remote(total.at[c, k - 1], chip_in.at[c, k - 1], chip_sem.at[l, c, k - 1], peer[2 * k])
                copy.start()
                chip.append(copy)

        for c in range(n_d):
            ffn_copy(l, 2 * n_d + c).wait()
            y = dot(act[...], buf[ffn_at(l, (2 * n_d + c) * pad_width, width), :])
            y = y.reshape(4, 2, n_rows, CHUNK)
            theirs = y[:, 1].reshape(4 * n_rows, CHUNK)
            for j in range(n_j):
                outbox[2 * c + j // 2, pl.ds(j % 2 * 4 * n_rows, 4 * n_rows), :] = theirs[:, j * 128:(j + 1) * 128]
            mine = y[:, 0].reshape(4 * n_rows, CHUNK)
            for j in range(n_j):
                qo[j, pl.ds(c * 4 * n_rows, 4 * n_rows), :] = mine[:, j * 128:(j + 1) * 128]
            copy = remote(outbox.at[pl.ds(2 * c, 2)], pair_in.at[pl.ds(2 * c, 2)], pair_sem.at[l, c], peer[1])
            copy.start()
            pair.append(copy)
            if c >= 1:
                reduce_chunk(c - 1)
        reduce_chunk(n_d - 1)
        if l + 1 < n_layers:
            start(kv_copy(l + 1, b) for b in range(n_rows))
            start(wo_copy(l + 1, n) for n in range(n_d))
        else:
            start(head_copy(i) for i in range(HEAD_B, HEAD_A))
        for copy in chip:
            copy.wait_recv()
        for c in range(n_d):
            cols = pl.ds(c * CHUNK, CHUNK)
            y = jnp.concatenate([qo[j, pl.ds(c * 4 * n_rows, n_rows), :] for j in range(n_j)], axis=1)
            for k in range(3):
                y = y + chip_in[c, k].astype(F32)
            x_cur[:, cols] = (x_cur[:, cols].astype(F32) + y).astype(BF16)
        for copy in sent + pair + chip:
            copy.wait_send()

    hrows[0] = rms_norm(x_cur[...], gain_fin[...])
    rows[me] = hrows[0]
    peer[0] = me
    sends = gather(hrows.at[0], lambda j, k: rows.at[peer[j]], fin_sem)
    for copy in sends:
        copy.wait_send()
    for i in range(n_vocab):
        head_copy(i).wait()


def head_kernel(dims, rows, buf, out_hbm, tile, sem):
    d_model, vocab = dims
    n_vocab = vocab // CHUNK

    def out_copy(i, cols, slot):
        at = pl.ds(i * 2 * CHUNK if isinstance(i, int) else pl.multiple_of(i * 2 * CHUNK, 128), cols)
        return pltpu.make_async_copy(tile.at[slot, :, pl.ds(0, cols)], out_hbm.at[:, at], sem.at[slot])

    def weights(chunk):
        return buf[pl.ds(pl.multiple_of(head_chunk(chunk) * d_model, 128), d_model), :]

    def step(i, carry):
        slot = lax.rem(i, 2)
        both = dot(rows[...], jnp.concatenate([weights(2 * i), weights(2 * i + 1)], axis=1))

        @pl.when(i >= 2)
        def _():
            out_copy(i - 2, 2 * CHUNK, slot).wait()

        tile[slot] = both
        out_copy(i, 2 * CHUNK, slot).start()
        return carry

    n_pairs = n_vocab // 2
    lax.fori_loop(0, n_pairs, step, 0)
    for i in (n_pairs - 2, n_pairs - 1):
        if i % 2 == n_pairs % 2:
            out_copy(i, 2 * CHUNK, i % 2).wait()
    if n_vocab % 2:
        tile[n_pairs % 2, :, pl.ds(0, CHUNK)] = dot(rows[...], weights(n_vocab - 1))
        out_copy(n_pairs, CHUNK, n_pairs % 2).start()
    out_copy(n_pairs - 1, 2 * CHUNK, (n_pairs - 1) % 2).wait()
    if n_vocab % 2:
        out_copy(n_pairs, CHUNK, n_pairs % 2).wait()


def run_head(rows, buf, vocab):
    n_rows, d_model = rows.shape
    vmem = pl.BlockSpec(memory_space=pltpu.VMEM)
    buf = pltpu.with_memory_space_constraint(buf, pltpu.VMEM)
    return pl.pallas_call(
        functools.partial(head_kernel, (d_model, vocab)),
        out_shape=jax.ShapeDtypeStruct((n_rows, vocab), F32),
        in_specs=[vmem, vmem],
        out_specs=pl.BlockSpec(memory_space=pl.ANY),
        scratch_shapes=[pltpu.VMEM((2, n_rows, 2 * CHUNK), F32), pltpu.SemaphoreType.DMA((2,))],
        compiler_params=pltpu.CompilerParams(vmem_limit_bytes=VMEM_LAYERS),
        name='head',
    )(rows, buf)


def run_layers(hidden, lengths, kv_t, gain_attn, w_q, w_o, gain_ffn, wg_t, wu_t, w_down, gain_fin, w_head):
    n_layers, n_rows, kv_width, seq_len = kv_t.shape
    d_model = hidden.shape[1]
    n_heads = w_q.shape[2] // kv_width
    width = w_down.shape[1]
    pad_width = round_up(width, 16)
    half, n_d = n_heads // 2, d_model // CHUNK
    n_q = half * kv_width // CHUNK
    n_t = round_up(kv_width, 128) // 128
    slot_rows = max(n_q * d_model, n_rows * kv_width, n_d * half * LATENT, 3 * n_d * pad_width)
    dims = (n_layers, n_rows, d_model, n_heads, kv_width, seq_len, width, pad_width, slot_rows, w_head.shape[1])
    vmem, anys = pl.BlockSpec(memory_space=pltpu.VMEM), pl.BlockSpec(memory_space=pl.ANY)
    smem = pl.BlockSpec(memory_space=pltpu.SMEM)
    dma = pltpu.SemaphoreType.DMA
    scratch = [
        pltpu.VMEM((n_rows, d_model), BF16),
        pltpu.VMEM((2, n_rows, d_model), BF16),
        pltpu.VMEM((n_t, n_heads * n_rows, 128), F32),
        pltpu.VMEM((8, half * n_rows, 128), F32),
        pltpu.VMEM((2, GROUP, n_heads, seq_len), BF16),
        pltpu.VMEM((2, half, n_rows, LATENT), BF16),
        pltpu.VMEM((half, n_rows, LATENT), BF16),
        pltpu.VMEM((n_d, CHUNK // 128 * n_rows, 128), F32),
        pltpu.VMEM((NUM_DEV * n_rows, width), BF16),
        pltpu.VMEM((8, half * n_rows, 128), F32),
        pltpu.VMEM((n_d, 3, n_rows, CHUNK), BF16),
        pltpu.VMEM((n_d, 3, n_rows, CHUNK), BF16),
        dma((n_layers, n_q)), dma((n_layers, n_rows)), dma((n_layers, n_d)), dma((n_layers, 3 * n_d)),
        dma((n_layers, 2)), dma((n_layers, half // 2, 2)), dma((n_layers, 2)), dma((n_layers, n_d, 2)),
        dma((n_layers, 8, 2)), dma((n_layers, n_d, 2)), dma((n_layers, n_d, 3, 2)), dma((8, 2)), dma((w_head.shape[1] // CHUNK,)),
    ]
    return pl.pallas_call(
        functools.partial(layers_kernel, dims),
        out_shape=[pltpu.VMEM((NUM_DEV, n_rows, d_model), BF16), pltpu.VMEM((3 * slot_rows, CHUNK), BF16)],
        in_specs=[vmem, smem, vmem, vmem, vmem] + [anys] * 7,
        out_specs=[vmem, vmem],
        scratch_shapes=scratch,
        compiler_params=pltpu.CompilerParams(collective_id=0, has_side_effects=True, vmem_limit_bytes=VMEM_LAYERS),
        name='layers',
    )(hidden, lengths, gain_attn, gain_ffn, gain_fin.reshape(1, -1), kv_t, w_q, w_o, wg_t, wu_t, w_down, w_head)


def solution(mesh):
    row_axes = ('rep', 'dp')
    specs_in = (P(row_axes, None), P(row_axes), P(None, row_axes, None, None), P(), P(), P(), P(),
                P(None, None, 'dp'), P(None, None, 'dp'), P(None, 'dp', None), P(), P(None, 'dp'))

    def device_step(hidden, lengths, kv_cache, norm_attn, w_q, w_o, norm_ffn, w_gate, w_up, w_down, norm_final, w_head):
        rows, buf = run_layers(hidden, lengths, jnp.swapaxes(kv_cache, 2, 3), norm_attn, w_q, w_o, norm_ffn,
                               jnp.swapaxes(w_gate, 1, 2), jnp.swapaxes(w_up, 1, 2), w_down, norm_final, w_head)
        return run_head(rows.reshape(-1, hidden.shape[1]), buf, w_head.shape[1])

    return jax.shard_map(device_step, mesh=mesh, in_specs=specs_in, out_specs=P('rep', 'dp'), check_vma=False)
```

time: 145 us -> 122 us (0.84)
  matrix products: 27.2 us -> 0 us
  Pallas kernels: 118 us -> 121 us
    dot_general x1 -> x0, matrix products: 27.2 us -> none  [dot(): return jnp.dot(a, b, preferred_element_type=F32)]
    pallas_call x1 -> x2, Pallas kernels: 118 us -> 121 us  [the longest x1 102 us: run_layers(): pl.pallas_call(functools.partial(layers_kernel, dims), out_shape=[pltpu.V...]
where the time goes in v3:
time: 122 us
  Pallas kernels  121 us (99%)
    pallas_call x1, Pallas kernels, run_layers(): pl.pallas_call(functools.partial(layers_kernel, dims), out_shape=[pltpu.V...  102 us
    pallas_call x1, Pallas kernels, run_head(): pl.pallas_call(functools.partial(head_kernel, (d_model, vocab)), out_shap...  18.8 us

profile of v3, /device:TPU:0, one launch (start us, length us, event | category | flops | bytes accessed | tf_op | source)
XLA Modules:
  0.0 122.1 jit_solution(7446856427072794646)
XLA Ops:
  0.0 102.2 %layers.1 = (bf16[8,32,2048]{2,1,0:T(8,128)(2,1)S(1)}, bf16[55296,512]{1,0:T(8,128)(2,1)S(1)}) custom-call(bf16[32,2048]{1,0:T(8,128)(2,1)} %x_ref.1, s32[32]{0:T(128)} %len_ref.1, f32[2,2048]{1,0:T(2,128)} %gain_attn.1, f32[2,2048]{1,0:T(2,128)} %gain_ffn.1, f32[1,2048]{1,0:T(1,128)} %bitcast.9, bf16[2,32,576,512]{3,2,1,0:T(8,128)(2,1)} %bitcast.6, ...), custom_call_target="tpu_custom_call" | custom-call | tf_op jit(solution)/shard_map/layers/pallas_call | solution.py:394
  102.2 0.0 copy-start
  102.2 1.0 copy-done
  103.1 18.8 %head.1 = f32[256,12800]{1,0:T(8,128)} custom-call(bf16[256,2048]{1,0:T(8,128)(2,1)} %bitcast.5, bf16[55296,512]{1,0:T(8,128)(2,1)S(1)} %get-tuple-element.8.buf), custom_call_target="tpu_custom_call" | custom-call | tf_op jit(solution)/shard_map/head/pallas_call | solution.py:352
Async XLA Ops:
  102.2 1.0 copy-start

commit v4 on v3

--- a/solution.py
+++ b/solution.py
@@ -97,16 +97,41 @@
         for copy in copies:
             copy.start()
 
-    def gather(own, slot_of, sems):
-        sends = {j: remote(own, slot_of(0, j), sems.at[j], peer[j]) for j in (6, 2, 4, 1)}
-        start(sends.values())
-        for j in (2, 4, 6):
-            sends[j].wait_recv()
-            sends[j + 1] = remote(slot_of(j, j), slot_of(j, j + 1), sems.at[j + 1], peer[1])
-            sends[j + 1].start()
-        for j in (1, 3, 5, 7):
-            sends[j].wait_recv()
-        return list(sends.values())
+    def gather(own, block, sems):
+        every, size = [], n_rows // 4
+        chunk = lambda ref, c: ref.at[pl.ds(c * size, size)]
+
+        def send(src, j, k):
+            copy = remote(src, block(j, k), sems.at[len(every)], peer[k])
+            copy.start()
+            every.append(copy)
+            return copy
+
+        def send_chunk(src, c, j, k):
+            copy = remote(chunk(src, c), chunk(block(j, k), c), sems.at[len(every)], peer[k])
+            copy.start()
+            every.append(copy)
+            return copy
+
+        x_order, y_order = (0, 1, 2, 3), (2, 3, 0, 1)
+        near = {}
+        for cx, cy in zip(x_order, y_order):
+            near[2, cx] = send_chunk(own, cx, 0, 2)
+            near[4, cy] = send_chunk(own, cy, 0, 4)
+        arrivals = [send(own, 0, 1)]
+        far = {}
+        for i in range(4):
+            for j, c in ((2, x_order[i]), (4, y_order[i])):
+                near[j, c].wait_recv()
+                if i < 2:
+                    far[c] = send_chunk(block(j, 0), c, j, 6 - j)
+                arrivals.append(send_chunk(block(j, 0), c, j, 1))
+        for c in (0, 2, 1, 3):
+            far[c].wait_recv()
+            arrivals.append(send_chunk(block(6, 0), c, 6, 1))
+        for copy in arrivals:
+            copy.wait_recv()
+        return every
 
     start(wq_copy(0, n) for n in range(n_q))
     x_cur[...] = x_ref[...]
@@ -234,7 +259,7 @@
             x_cur[:, cols] = (x_cur[:, cols].astype(F32) + (own[n] + theirs)).astype(BF16)
 
         rows[0] = rms_norm(x_cur[...], gain_ffn[pl.ds(l, 1), :])
-        row_sends = gather(rows.at[0], lambda j, k: rows.at[k], ag_sem.at[l])
+        row_sends = gather(rows.at[0], lambda j, k: rows.at[j ^ k], ag_sem.at[l])
         if l + 1 < n_layers:
             start(wq_copy(l + 1, n) for n in range(n_q))
         for i in range(2 * n_d):
@@ -249,7 +274,8 @@
 
         for copy in row_sends + p_copies:
             copy.wait_send()
-        pair, chip = [], []
+        pair, chip, relay = [], [], []
+        first, second = (1, 2, 1, 2), (2, 1, 2, 1)
 
         def reduce_chunk(c):
             pair[c].wait_recv()
@@ -258,14 +284,24 @@
                 for j in range(n_j):
                     lanes = pl.ds(j * 128, 128)
                     both = qo[j, at, :] + pair_in[2 * c + j // 2, pl.ds((j % 2 * 4 + k) * n_rows, n_rows), :]
-                    if k == 0:
+                    if k in (0, second[c]):
                         qo[j, at, :] = both
                     else:
-                        total[c, k - 1, :, lanes] = both.astype(BF16)
-            for k in (3, 1, 2):
-                copy = remote(total.at[c, k - 1], chip_in.at[c, k - 1], chip_sem.at[l, c, k - 1], peer[2 * k])
+                        total[c, k // 3, :, lanes] = both.astype(BF16)
+            for i in (1, 0):
+                copy = remote(total.at[c, i], chip_in.at[c, i], chip_sem.at[l, c, i], peer[2 * first[c]])
                 copy.start()
                 chip.append(copy)
+
+        def relay_chunk(c):
+            chip[2 * c].wait_recv()
+            at = pl.ds((c * 4 + second[c]) * n_rows, n_rows)
+            for j in range(n_j):
+                lanes = pl.ds(j * 128, 128)
+                total[c, 2, :, lanes] = (qo[j, at, :] + chip_in[c, 1, :, lanes].astype(F32)).astype(BF16)
+            copy = remote(total.at[c, 2], chip_in.at[c, 2], chip_sem.at[l, c, 2], peer[2 * second[c]])
+            copy.start()
+            relay.append(copy)
 
         for c in range(n_d):
             ffn_copy(l, 2 * n_d + c).wait()
@@ -283,20 +319,22 @@
             if c >= 1:
                 reduce_chunk(c - 1)
         reduce_chunk(n_d - 1)
+        for c in range(n_d):
+            relay_chunk(c)
         if l + 1 < n_layers:
             start(kv_copy(l + 1, b) for b in range(n_rows))
             start(wo_copy(l + 1, n) for n in range(n_d))
         else:
             start(head_copy(i) for i in range(HEAD_B, HEAD_A))
-        for copy in chip:
+        for copy in chip[1::2] + relay:
             copy.wait_recv()
         for c in range(n_d):
             cols = pl.ds(c * CHUNK, CHUNK)
             y = jnp.concatenate([qo[j, pl.ds(c * 4 * n_rows, n_rows), :] for j in range(n_j)], axis=1)
-            for k in range(3):
-                y = y + chip_in[c, k].astype(F32)
+            for i in (0, 2):
+                y = y + chip_in[c, i].astype(F32)
             x_cur[:, cols] = (x_cur[:, cols].astype(F32) + y).astype(BF16)
-        for copy in sent + pair + chip:
+        for copy in sent + pair + chip + relay:
             copy.wait_send()
 
     hrows[0] = rms_norm(x_cur[...], gain_fin[...])
@@ -321,40 +359,43 @@
         return buf[pl.ds(pl.multiple_of(head_chunk(chunk) * d_model, 128), d_model), :]
 
     def step(i, carry):
-        slot = lax.rem(i, 2)
-        both = dot(rows[...], jnp.concatenate([weights(2 * i), weights(2 * i + 1)], axis=1))
+        half = lax.rem(i, 2) * 2
 
         @pl.when(i >= 2)
         def _():
-            out_copy(i - 2, 2 * CHUNK, slot).wait()
-
-        tile[slot] = both
-        out_copy(i, 2 * CHUNK, slot).start()
+            for h in (0, 1):
+                out_copy(2 * i - 4 + h, 2 * CHUNK, half + h).wait()
+
+        for c in range(4):
+            tile[half + c // 2, :, pl.ds(c % 2 * CHUNK, CHUNK)] = dot(x, weights(4 * i + c))
+        for h in (0, 1):
+            out_copy(2 * i + h, 2 * CHUNK, half + h).start()
         return carry
 
-    n_pairs = n_vocab // 2
-    lax.fori_loop(0, n_pairs, step, 0)
-    for i in (n_pairs - 2, n_pairs - 1):
-        if i % 2 == n_pairs % 2:
-            out_copy(i, 2 * CHUNK, i % 2).wait()
-    if n_vocab % 2:
-        tile[n_pairs % 2, :, pl.ds(0, CHUNK)] = dot(rows[...], weights(n_vocab - 1))
-        out_copy(n_pairs, CHUNK, n_pairs % 2).start()
-    out_copy(n_pairs - 1, 2 * CHUNK, (n_pairs - 1) % 2).wait()
-    if n_vocab % 2:
-        out_copy(n_pairs, CHUNK, n_pairs % 2).wait()
+    x = rows[...].reshape(-1, d_model)
+    n_quads = n_vocab // 4
+    lax.fori_loop(0, n_quads, step, 0)
+    for i in range(max(n_quads - 2, 0), n_quads):
+        for h in (0, 1):
+            out_copy(2 * i + h, 2 * CHUNK, i % 2 * 2 + h).wait()
+        if i == n_quads - 2 and n_vocab % 4:
+            last = n_quads % 2 * 2
+            tile[last, :, pl.ds(0, CHUNK)] = dot(x, weights(n_vocab - 1))
+            out_copy(2 * n_quads, CHUNK, last).start()
+    if n_vocab % 4:
+        out_copy(2 * n_quads, CHUNK, n_quads % 2 * 2).wait()
 
 
 def run_head(rows, buf, vocab):
-    n_rows, d_model = rows.shape
+    n_rows, d_model = rows.shape[0] * rows.shape[1], rows.shape[2]
     vmem = pl.BlockSpec(memory_space=pltpu.VMEM)
-    buf = pltpu.with_memory_space_constraint(buf, pltpu.VMEM)
+    rows, buf = (pltpu.with_memory_space_constraint(a, pltpu.VMEM) for a in (rows, buf))
     return pl.pallas_call(
         functools.partial(head_kernel, (d_model, vocab)),
         out_shape=jax.ShapeDtypeStruct((n_rows, vocab), F32),
         in_specs=[vmem, vmem],
         out_specs=pl.BlockSpec(memory_space=pl.ANY),
-        scratch_shapes=[pltpu.VMEM((2, n_rows, 2 * CHUNK), F32), pltpu.SemaphoreType.DMA((2,))],
+        scratch_shapes=[pltpu.VMEM((4, n_rows, 2 * CHUNK), F32), pltpu.SemaphoreType.DMA((4,))],
         compiler_params=pltpu.CompilerParams(vmem_limit_bytes=VMEM_LAYERS),
         name='head',
     )(rows, buf)
@@ -389,7 +430,7 @@
         pltpu.VMEM((n_d, 3, n_rows, CHUNK), BF16),
         dma((n_layers, n_q)), dma((n_layers, n_rows)), dma((n_layers, n_d)), dma((n_layers, 3 * n_d)),
         dma((n_layers, 2)), dma((n_layers, half // 2, 2)), dma((n_layers, 2)), dma((n_layers, n_d, 2)),
-        dma((n_layers, 8, 2)), dma((n_layers, n_d, 2)), dma((n_layers, n_d, 3, 2)), dma((8, 2)), dma((w_head.shape[1] // CHUNK,)),
+        dma((n_layers, 25, 2)), dma((n_layers, n_d, 2)), dma((n_layers, n_d, 3, 2)), dma((25, 2)), dma((w_head.shape[1] // CHUNK,)),
     ]
     return pl.pallas_call(
         functools.partial(layers_kernel, dims),
@@ -410,6 +451,6 @@
     def device_step(hidden, lengths, kv_cache, norm_attn, w_q, w_o, norm_ffn, w_gate, w_up, w_down, norm_final, w_head):
         rows, buf = run_layers(hidden, lengths, jnp.swapaxes(kv_cache, 2, 3), norm_attn, w_q, w_o, norm_ffn,
                                jnp.swapaxes(w_gate, 1, 2), jnp.swapaxes(w_up, 1, 2), w_down, norm_final, w_head)
-        return run_head(rows.reshape(-1, hidden.shape[1]), buf, w_head.shape[1])
+        return run_head(rows, buf, w_head.shape[1])
 
     return jax.shard_map(device_step, mesh=mesh, in_specs=specs_in, out_specs=P('rep', 'dp'), check_vma=False)

time: 122 us -> 117 us (0.959)
  Pallas kernels: 121 us -> 117 us
    pallas_call x1, Pallas kernels: 18.8 us -> 15.8 us  [run_head(): pl.pallas_call(functools.partial(head_kernel, (d_model, vocab)), out_shap...]
    pallas_call x1, Pallas kernels: 102 us -> 101 us  [run_layers(): pl.pallas_call(functools.partial(layers_kernel, dims), out_shape=[pltpu.V...]
where the time goes in v4:
time: 117 us
  Pallas kernels  117 us (100%)
    pallas_call x1, Pallas kernels, run_layers(): pl.pallas_call(functools.partial(layers_kernel, dims), out_shape=[pltpu.V...  101 us
    pallas_call x1, Pallas kernels, run_head(): pl.pallas_call(functools.partial(head_kernel, (d_model, vocab)), out_shap...  15.8 us

profile of v4, /device:TPU:0, one launch (start us, length us, event | category | flops | bytes accessed | tf_op | source)
XLA Modules:
  0.0 116.9 jit_solution(13805302698592385346)
XLA Ops:
  0.0 100.9 %layers.1 = (bf16[8,32,2048]{2,1,0:T(8,128)(2,1)S(1)}, bf16[55296,512]{1,0:T(8,128)(2,1)S(1)}) custom-call(bf16[32,2048]{1,0:T(8,128)(2,1)} %x_ref.1, s32[32]{0:T(128)} %len_ref.1, f32[2,2048]{1,0:T(2,128)} %gain_attn.1, f32[2,2048]{1,0:T(2,128)} %gain_ffn.1, f32[1,2048]{1,0:T(1,128)} %bitcast.7, bf16[2,32,576,512]{3,2,1,0:T(8,128)(2,1)} %bitcast.4, ...), custom_call_target="tpu_custom_call" | custom-call | tf_op jit(solution)/shard_map/layers/pallas_call | solution.py:435
  100.9 15.8 %head.1 = f32[256,12800]{1,0:T(8,128)} custom-call(bf16[8,32,2048]{2,1,0:T(8,128)(2,1)S(1)} %get-tuple-element.7.rows, bf16[55296,512]{1,0:T(8,128)(2,1)S(1)} %get-tuple-element.8.buf), custom_call_target="tpu_custom_call" | custom-call | tf_op jit(solution)/shard_map/head/pallas_call | solution.py:393

commit v5 on v4

--- a/solution.py
+++ b/solution.py
@@ -12,7 +12,7 @@
 NORM_EPS = 1e-6
 MESH_ID = pl.DeviceIdType.MESH
 NUM_DEV = 8
-CHUNK = 512
+CHUNK, RS_CHUNK = 512, 256
 GROUP = 8
 HEAD_A, HEAD_B = 16, 9
 VMEM_LAYERS = int(8.9 * 2**20)
@@ -150,15 +150,17 @@
         copy.wait_recv()
         both_rows = hrows[...].reshape(2 * n_rows, d_model)
         prev, q_copies = None, []
-        for first in range(0, n_q, 3):
-            for n in range(first, first + 3):
+        bounds = [(i, min(i + 3, n_q)) for i in range(0, n_q, 3)]
+        if l == 0:
+            bounds[-1:] = [(n_q - 3, n_q - 1), (n_q - 1, n_q)]
+        for first, stop in bounds:
+            for n in range(first, stop):
                 wq_copy(l, n).wait()
             if l == 0:
-                per = -(-3 * n_rows // n_q)
-                start(kv_copy(l, b) for b in range(first // 3 * per, min((first // 3 + 1) * per, n_rows)))
-            weights = jnp.concatenate([buf[wq_at(l, n * d_model, d_model), :] for n in range(first, first + 3)], axis=1)
+                start(kv_copy(l, b) for b in range(first * n_rows // n_q, stop * n_rows // n_q))
+            weights = jnp.concatenate([buf[wq_at(l, n * d_model, d_model), :] for n in range(first, stop)], axis=1)
             wide = dot(both_rows, weights).astype(BF16).astype(F32)
-            for n in range(first, first + 3):
+            for n in range(first, stop):
                 cur = wide[:, (n - first) * CHUNK:(n - first + 1) * CHUNK]
                 if n >= 1:
                     h = n - 1
@@ -275,19 +277,21 @@
         for copy in row_sends + p_copies:
             copy.wait_send()
         pair, chip, relay = [], [], []
-        first, second = (1, 2, 1, 2), (2, 1, 2, 1)
+        n_r, n_i = d_model // RS_CHUNK, RS_CHUNK // 128
+        first = [1 + c % 2 for c in range(n_r)]
+        second = [3 - k for k in first]
+        kept = lambda c, i, k, n: (n_i * (c // 4) + i, pl.ds((c % 4 * 4 + k) * n_rows, n * n_rows))
 
         def reduce_chunk(c):
             pair[c].wait_recv()
             for k in range(4):
-                at = pl.ds((c * 4 + k) * n_rows, n_rows)
-                for j in range(n_j):
-                    lanes = pl.ds(j * 128, 128)
-                    both = qo[j, at, :] + pair_in[2 * c + j // 2, pl.ds((j % 2 * 4 + k) * n_rows, n_rows), :]
+                for i in range(n_i):
+                    at = kept(c, i, k, 1)
+                    both = qo[at[0], at[1], :] + pair_in[c, pl.ds((i * 4 + k) * n_rows, n_rows), :]
                     if k in (0, second[c]):
-                        qo[j, at, :] = both
+                        qo[at[0], at[1], :] = both
                     else:
-                        total[c, k // 3, :, lanes] = both.astype(BF16)
+                        total[c, k // 3, :, pl.ds(i * 128, 128)] = both.astype(BF16)
             for i in (1, 0):
                 copy = remote(total.at[c, i], chip_in.at[c, i], chip_sem.at[l, c, i], peer[2 * first[c]])
                 copy.start()
@@ -295,42 +299,45 @@
 
         def relay_chunk(c):
             chip[2 * c].wait_recv()
-            at = pl.ds((c * 4 + second[c]) * n_rows, n_rows)
-            for j in range(n_j):
-                lanes = pl.ds(j * 128, 128)
-                total[c, 2, :, lanes] = (qo[j, at, :] + chip_in[c, 1, :, lanes].astype(F32)).astype(BF16)
+            for i in range(n_i):
+                at, lanes = kept(c, i, second[c], 1), pl.ds(i * 128, 128)
+                total[c, 2, :, lanes] = (qo[at[0], at[1], :] + chip_in[c, 1, :, lanes].astype(F32)).astype(BF16)
             copy = remote(total.at[c, 2], chip_in.at[c, 2], chip_sem.at[l, c, 2], peer[2 * second[c]])
             copy.start()
             relay.append(copy)
 
-        for c in range(n_d):
-            ffn_copy(l, 2 * n_d + c).wait()
-            y = dot(act[...], buf[ffn_at(l, (2 * n_d + c) * pad_width, width), :])
-            y = y.reshape(4, 2, n_rows, CHUNK)
-            theirs = y[:, 1].reshape(4 * n_rows, CHUNK)
-            for j in range(n_j):
-                outbox[2 * c + j // 2, pl.ds(j % 2 * 4 * n_rows, 4 * n_rows), :] = theirs[:, j * 128:(j + 1) * 128]
-            mine = y[:, 0].reshape(4 * n_rows, CHUNK)
-            for j in range(n_j):
-                qo[j, pl.ds(c * 4 * n_rows, 4 * n_rows), :] = mine[:, j * 128:(j + 1) * 128]
-            copy = remote(outbox.at[pl.ds(2 * c, 2)], pair_in.at[pl.ds(2 * c, 2)], pair_sem.at[l, c], peer[1])
+        for c in range(n_r):
+            n, col = c * RS_CHUNK // CHUNK, c * RS_CHUNK % CHUNK
+            if col == 0:
+                ffn_copy(l, 2 * n_d + n).wait()
+            y = dot(act[...], buf[ffn_at(l, (2 * n_d + n) * pad_width, width), pl.ds(col, RS_CHUNK)])
+            y = y.reshape(4, 2, n_rows, RS_CHUNK)
+            theirs, mine = (y[:, i].reshape(4 * n_rows, RS_CHUNK) for i in (1, 0))
+            for i in range(n_i):
+                outbox[c, pl.ds(i * 4 * n_rows, 4 * n_rows), :] = theirs[:, i * 128:(i + 1) * 128]
+            copy = remote(outbox.at[c], pair_in.at[c], pair_sem.at[l, c], peer[1])
             copy.start()
             pair.append(copy)
-            if c >= 1:
-                reduce_chunk(c - 1)
-        reduce_chunk(n_d - 1)
-        for c in range(n_d):
-            relay_chunk(c)
+            for i in range(n_i):
+                at = kept(c, i, 0, 4)
+                qo[at[0], at[1], :] = mine[:, i * 128:(i + 1) * 128]
+            if c >= 2:
+                reduce_chunk(c - 2)
+        for c in (n_r - 2, n_r - 1):
+            reduce_chunk(c)
         if l + 1 < n_layers:
             start(kv_copy(l + 1, b) for b in range(n_rows))
             start(wo_copy(l + 1, n) for n in range(n_d))
         else:
             start(head_copy(i) for i in range(HEAD_B, HEAD_A))
-        for copy in chip[1::2] + relay:
-            copy.wait_recv()
-        for c in range(n_d):
-            cols = pl.ds(c * CHUNK, CHUNK)
-            y = jnp.concatenate([qo[j, pl.ds(c * 4 * n_rows, n_rows), :] for j in range(n_j)], axis=1)
+        for c in range(n_r):
+            relay_chunk(c)
+        for c in range(n_r):
+            cols = pl.ds(c * RS_CHUNK, RS_CHUNK)
+            chip[2 * c + 1].wait_recv()
+            relay[c].wait_recv()
+            at = [kept(c, i, 0, 1) for i in range(n_i)]
+            y = jnp.concatenate([qo[t, r, :] for t, r in at], axis=1)
             for i in (0, 2):
                 y = y + chip_in[c, i].astype(F32)
             x_cur[:, cols] = (x_cur[:, cols].astype(F32) + y).astype(BF16)
@@ -407,7 +414,7 @@
     n_heads = w_q.shape[2] // kv_width
     width = w_down.shape[1]
     pad_width = round_up(width, 16)
-    half, n_d = n_heads // 2, d_model // CHUNK
+    half, n_d, n_r = n_heads // 2, d_model // CHUNK, d_model // RS_CHUNK
     n_q = half * kv_width // CHUNK
     n_t = round_up(kv_width, 128) // 128
     slot_rows = max(n_q * d_model, n_rows * kv_width, n_d * half * LATENT, 3 * n_d * pad_width)
@@ -419,18 +426,18 @@
         pltpu.VMEM((n_rows, d_model), BF16),
         pltpu.VMEM((2, n_rows, d_model), BF16),
         pltpu.VMEM((n_t, n_heads * n_rows, 128), F32),
-        pltpu.VMEM((8, half * n_rows, 128), F32),
+        pltpu.VMEM((n_r, half * n_rows, 128), F32),
         pltpu.VMEM((2, GROUP, n_heads, seq_len), BF16),
         pltpu.VMEM((2, half, n_rows, LATENT), BF16),
         pltpu.VMEM((half, n_rows, LATENT), BF16),
         pltpu.VMEM((n_d, CHUNK // 128 * n_rows, 128), F32),
         pltpu.VMEM((NUM_DEV * n_rows, width), BF16),
-        pltpu.VMEM((8, half * n_rows, 128), F32),
-        pltpu.VMEM((n_d, 3, n_rows, CHUNK), BF16),
-        pltpu.VMEM((n_d, 3, n_rows, CHUNK), BF16),
+        pltpu.VMEM((n_r, half * n_rows, 128), F32),
+        pltpu.VMEM((n_r, 3, n_rows, RS_CHUNK), BF16),
+        pltpu.VMEM((n_r, 3, n_rows, RS_CHUNK), BF16),
         dma((n_layers, n_q)), dma((n_layers, n_rows)), dma((n_layers, n_d)), dma((n_layers, 3 * n_d)),
         dma((n_layers, 2)), dma((n_layers, half // 2, 2)), dma((n_layers, 2)), dma((n_layers, n_d, 2)),
-        dma((n_layers, 25, 2)), dma((n_layers, n_d, 2)), dma((n_layers, n_d, 3, 2)), dma((25, 2)), dma((w_head.shape[1] // CHUNK,)),
+        dma((n_layers, 25, 2)), dma((n_layers, n_r, 2)), dma((n_layers, n_r, 3, 2)), dma((25, 2)), dma((w_head.shape[1] // CHUNK,)),
     ]
     return pl.pallas_call(
         functools.partial(layers_kernel, dims),

time: 117 us -> 120 us (1.026)
  Pallas kernels: 117 us -> 119 us
    pallas_call x1, Pallas kernels: 101 us -> 104 us  [run_layers(): pl.pallas_call(functools.partial(layers_kernel, dims), out_shape=[pltpu.V...]
where the time goes in v5:
time: 120 us
  Pallas kernels  119 us (99%)
    pallas_call x1, Pallas kernels, run_layers(): pl.pallas_call(functools.partial(layers_kernel, dims), out_shape=[pltpu.V...  104 us
    pallas_call x1, Pallas kernels, run_head(): pl.pallas_call(functools.partial(head_kernel, (d_model, vocab)), out_shap...  15.8 us

profile of v5, /device:TPU:0, one launch (start us, length us, event | category | flops | bytes accessed | tf_op | source)
XLA Modules:
  0.0 119.6 jit_solution(13353709976439921449)
XLA Ops:
  0.0 103.6 %layers.1 = (bf16[8,32,2048]{2,1,0:T(8,128)(2,1)S(1)}, bf16[55296,512]{1,0:T(8,128)(2,1)S(1)}) custom-call(bf16[32,2048]{1,0:T(8,128)(2,1)} %x_ref.1, s32[32]{0:T(128)} %len_ref.1, f32[2,2048]{1,0:T(2,128)} %gain_attn.1, f32[2,2048]{1,0:T(2,128)} %gain_ffn.1, f32[1,2048]{1,0:T(1,128)} %bitcast.7, bf16[2,32,576,512]{3,2,1,0:T(8,128)(2,1)} %bitcast.4, ...), custom_call_target="tpu_custom_call" | custom-call | tf_op jit(solution)/shard_map/layers/pallas_call | solution.py:442
  103.6 15.8 %head.1 = f32[256,12800]{1,0:T(8,128)} custom-call(bf16[8,32,2048]{2,1,0:T(8,128)(2,1)S(1)} %get-tuple-element.7.rows, bf16[55296,512]{1,0:T(8,128)(2,1)S(1)} %get-tuple-element.8.buf), custom_call_target="tpu_custom_call" | custom-call | tf_op jit(solution)/shard_map/head/pallas_call | solution.py:400

commit v6 on v4

--- a/solution.py
+++ b/solution.py
@@ -274,8 +274,7 @@
 
         for copy in row_sends + p_copies:
             copy.wait_send()
-        pair, chip, relay = [], [], []
-        first, second = (1, 2, 1, 2), (2, 1, 2, 1)
+        pair, chip = [], []
 
         def reduce_chunk(c):
             pair[c].wait_recv()
@@ -284,24 +283,14 @@
                 for j in range(n_j):
                     lanes = pl.ds(j * 128, 128)
                     both = qo[j, at, :] + pair_in[2 * c + j // 2, pl.ds((j % 2 * 4 + k) * n_rows, n_rows), :]
-                    if k in (0, second[c]):
+                    if k == 0:
                         qo[j, at, :] = both
                     else:
-                        total[c, k // 3, :, lanes] = both.astype(BF16)
-            for i in (1, 0):
-                copy = remote(total.at[c, i], chip_in.at[c, i], chip_sem.at[l, c, i], peer[2 * first[c]])
+                        total[c, k - 1, :, lanes] = both.astype(BF16)
+            for k in (3, 1, 2):
+                copy = remote(total.at[c, k - 1], chip_in.at[c, k - 1], chip_sem.at[l, c, k - 1], peer[2 * k])
                 copy.start()
                 chip.append(copy)
-
-        def relay_chunk(c):
-            chip[2 * c].wait_recv()
-            at = pl.ds((c * 4 + second[c]) * n_rows, n_rows)
-            for j in range(n_j):
-                lanes = pl.ds(j * 128, 128)
-                total[c, 2, :, lanes] = (qo[j, at, :] + chip_in[c, 1, :, lanes].astype(F32)).astype(BF16)
-            copy = remote(total.at[c, 2], chip_in.at[c, 2], chip_sem.at[l, c, 2], peer[2 * second[c]])
-            copy.start()
-            relay.append(copy)
 
         for c in range(n_d):
             ffn_copy(l, 2 * n_d + c).wait()
@@ -319,22 +308,20 @@
             if c >= 1:
                 reduce_chunk(c - 1)
         reduce_chunk(n_d - 1)
-        for c in range(n_d):
-            relay_chunk(c)
         if l + 1 < n_layers:
             start(kv_copy(l + 1, b) for b in range(n_rows))
             start(wo_copy(l + 1, n) for n in range(n_d))
         else:
             start(head_copy(i) for i in range(HEAD_B, HEAD_A))
-        for copy in chip[1::2] + relay:
-            copy.wait_recv()
         for c in range(n_d):
             cols = pl.ds(c * CHUNK, CHUNK)
+            for copy in chip[3 * c:3 * c + 3]:
+                copy.wait_recv()
             y = jnp.concatenate([qo[j, pl.ds(c * 4 * n_rows, n_rows), :] for j in range(n_j)], axis=1)
-            for i in (0, 2):
-                y = y + chip_in[c, i].astype(F32)
+            for k in range(3):
+                y = y + chip_in[c, k].astype(F32)
             x_cur[:, cols] = (x_cur[:, cols].astype(F32) + y).astype(BF16)
-        for copy in sent + pair + chip + relay:
+        for copy in sent + pair + chip:
             copy.wait_send()
 
     hrows[0] = rms_norm(x_cur[...], gain_fin[...])

time: 117 us -> 115 us (0.983)
  Pallas kernels: 117 us -> 115 us
    pallas_call x1, Pallas kernels: 101 us -> 99.3 us  [run_layers(): pl.pallas_call(functools.partial(layers_kernel, dims), out_shape=[pltpu.V...]
where the time goes in v6:
time: 115 us
  Pallas kernels  115 us (100%)
    pallas_call x1, Pallas kernels, run_layers(): pl.pallas_call(functools.partial(layers_kernel, dims), out_shape=[pltpu.V...  99.3 us
    pallas_call x1, Pallas kernels, run_head(): pl.pallas_call(functools.partial(head_kernel, (d_model, vocab)), out_shap...  15.8 us

profile of v6, /device:TPU:0, one launch (start us, length us, event | category | flops | bytes accessed | tf_op | source)
XLA Modules:
  0.0 115.4 jit_solution(13346980277075228209)
XLA Ops:
  0.0 99.3 %layers.1 = (bf16[8,32,2048]{2,1,0:T(8,128)(2,1)S(1)}, bf16[55296,512]{1,0:T(8,128)(2,1)S(1)}) custom-call(bf16[32,2048]{1,0:T(8,128)(2,1)} %x_ref.1, s32[32]{0:T(128)} %len_ref.1, f32[2,2048]{1,0:T(2,128)} %gain_attn.1, f32[2,2048]{1,0:T(2,128)} %gain_ffn.1, f32[1,2048]{1,0:T(1,128)} %bitcast.7, bf16[2,32,576,512]{3,2,1,0:T(8,128)(2,1)} %bitcast.4, ...), custom_call_target="tpu_custom_call" | custom-call | tf_op jit(solution)/shard_map/layers/pallas_call | solution.py:422
  99.3 15.8 %head.1 = f32[256,12800]{1,0:T(8,128)} custom-call(bf16[8,32,2048]{2,1,0:T(8,128)(2,1)S(1)} %get-tuple-element.7.rows, bf16[55296,512]{1,0:T(8,128)(2,1)S(1)} %get-tuple-element.8.buf), custom_call_target="tpu_custom_call" | custom-call | tf_op jit(solution)/shard_map/head/pallas_call | solution.py:380

commit v7 on v6

--- a/solution.py
+++ b/solution.py
@@ -45,9 +45,10 @@
     return [(lo, min(lo + CHUNK, width)) for lo in range(0, width, CHUNK)]
 
 
-def layers_kernel(dims, x_ref, len_ref, gain_attn, gain_ffn, gain_fin, kv_hbm, wq_hbm, wo_hbm, wg_hbm, wu_hbm, wd_hbm,
+def layers_kernel(dims, x_hbm, len_hbm, gain_attn_hbm, gain_ffn_hbm, gain_fin_hbm, kv_hbm, wq_hbm, wo_hbm, wg_hbm, wu_hbm, wd_hbm,
                   wh_hbm, rows, buf, x_cur, hrows, qo, outbox, p_buf, ol, ol_send, pr, act, pair_in, total, chip_in,
-                  wq_sem, kv_sem, wo_sem, ffn_sem, h_sem, q_sem, o_sem, p_sem, ag_sem, pair_sem, chip_sem, fin_sem, head_sem):
+                  wq_sem, kv_sem, wo_sem, ffn_sem, h_sem, q_sem, o_sem, p_sem, ag_sem, pair_sem, chip_sem, fin_sem, head_sem,
+                  len_ref, gain_attn, gain_ffn, gain_fin, in_sem):
     n_layers, n_rows, d_model, n_heads, kv_width, seq_len, width, pad_width, slot_rows, vocab = dims
     half = n_heads // 2
     q_cols = half * kv_width
@@ -134,7 +135,11 @@
         return every
 
     start(wq_copy(0, n) for n in range(n_q))
-    x_cur[...] = x_ref[...]
+    small = [pltpu.make_async_copy(src, dst, in_sem.at[i]) for i, (src, dst) in enumerate(
+        ((x_hbm, x_cur), (gain_attn_hbm, gain_attn), (gain_ffn_hbm, gain_ffn), (gain_fin_hbm, gain_fin), (len_hbm, len_ref)))]
+    start(small)
+    for copy in small:
+        copy.wait()
 
     for l in range(n_layers):
         sent = []
@@ -150,15 +155,17 @@
         copy.wait_recv()
         both_rows = hrows[...].reshape(2 * n_rows, d_model)
         prev, q_copies = None, []
-        for first in range(0, n_q, 3):
-            for n in range(first, first + 3):
+        bounds = [(i, min(i + 3, n_q)) for i in range(0, n_q, 3)]
+        if l == 0:
+            bounds[-1:] = [(n_q - 3, n_q - 1), (n_q - 1, n_q)]
+        for first, stop in bounds:
+            for n in range(first, stop):
                 wq_copy(l, n).wait()
             if l == 0:
-                per = -(-3 * n_rows // n_q)
-                start(kv_copy(l, b) for b in range(first // 3 * per, min((first // 3 + 1) * per, n_rows)))
-            weights = jnp.concatenate([buf[wq_at(l, n * d_model, d_model), :] for n in range(first, first + 3)], axis=1)
+                start(kv_copy(l, b) for b in range(first * n_rows // n_q, stop * n_rows // n_q))
+            weights = jnp.concatenate([buf[wq_at(l, n * d_model, d_model), :] for n in range(first, stop)], axis=1)
             wide = dot(both_rows, weights).astype(BF16).astype(F32)
-            for n in range(first, first + 3):
+            for n in range(first, stop):
                 cur = wide[:, (n - first) * CHUNK:(n - first + 1) * CHUNK]
                 if n >= 1:
                     h = n - 1
@@ -193,7 +200,7 @@
                 q = jnp.concatenate(q, axis=1)[:, :kv_width]
                 row = pl.multiple_of(b * kv_width, 64)
                 s = dot(q, buf[kv_at(l, row, kv_width), :]) * QK_SCALE
-                s = jnp.where(key_pos < len_ref[b], s, -1e30)
+                s = jnp.where(key_pos < len_ref[0, b], s, -1e30)
                 e = jnp.exp(s - jnp.max(s, axis=-1, keepdims=True))
                 p_buf[slot, i] = (e / jnp.sum(e, axis=-1, keepdims=True)).astype(BF16)
 
@@ -400,7 +407,6 @@
     slot_rows = max(n_q * d_model, n_rows * kv_width, n_d * half * LATENT, 3 * n_d * pad_width)
     dims = (n_layers, n_rows, d_model, n_heads, kv_width, seq_len, width, pad_width, slot_rows, w_head.shape[1])
     vmem, anys = pl.BlockSpec(memory_space=pltpu.VMEM), pl.BlockSpec(memory_space=pl.ANY)
-    smem = pl.BlockSpec(memory_space=pltpu.SMEM)
     dma = pltpu.SemaphoreType.DMA
     scratch = [
         pltpu.VMEM((n_rows, d_model), BF16),
@@ -418,16 +424,18 @@
         dma((n_layers, n_q)), dma((n_layers, n_rows)), dma((n_layers, n_d)), dma((n_layers, 3 * n_d)),
         dma((n_layers, 2)), dma((n_layers, half // 2, 2)), dma((n_layers, 2)), dma((n_layers, n_d, 2)),
         dma((n_layers, 25, 2)), dma((n_layers, n_d, 2)), dma((n_layers, n_d, 3, 2)), dma((25, 2)), dma((w_head.shape[1] // CHUNK,)),
+        pltpu.SMEM((1, n_rows), jnp.int32), pltpu.VMEM((n_layers, d_model), F32), pltpu.VMEM((n_layers, d_model), F32),
+        pltpu.VMEM((1, d_model), F32), dma((5,)),
     ]
     return pl.pallas_call(
         functools.partial(layers_kernel, dims),
         out_shape=[pltpu.VMEM((NUM_DEV, n_rows, d_model), BF16), pltpu.VMEM((3 * slot_rows, CHUNK), BF16)],
-        in_specs=[vmem, smem, vmem, vmem, vmem] + [anys] * 7,
+        in_specs=[anys] * 12,
         out_specs=[vmem, vmem],
         scratch_shapes=scratch,
         compiler_params=pltpu.CompilerParams(collective_id=0, has_side_effects=True, vmem_limit_bytes=VMEM_LAYERS),
         name='layers',
-    )(hidden, lengths, gain_attn, gain_ffn, gain_fin.reshape(1, -1), kv_t, w_q, w_o, wg_t, wu_t, w_down, w_head)
+    )(hidden, lengths.reshape(1, -1), gain_attn, gain_ffn, gain_fin.reshape(1, -1), kv_t, w_q, w_o, wg_t, wu_t, w_down, w_head)
 
 
 def solution(mesh):

time: 115 us -> 120 us (1.043)
  Pallas kernels: 115 us -> 120 us
    pallas_call x1, Pallas kernels: 99.3 us -> 104 us  [run_layers(): pl.pallas_call(functools.partial(layers_kernel, dims), out_shape=[pltpu.V...]
where the time goes in v7:
time: 120 us
  Pallas kernels  120 us (100%)
    pallas_call x1, Pallas kernels, run_layers(): pl.pallas_call(functools.partial(layers_kernel, dims), out_shape=[pltpu.V...  104 us
    pallas_call x1, Pallas kernels, run_head(): pl.pallas_call(functools.partial(head_kernel, (d_model, vocab)), out_shap...  15.8 us

profile of v7, /device:TPU:0, one launch (start us, length us, event | category | flops | bytes accessed | tf_op | source)
XLA Modules:
  0.0 119.8 jit_solution(4511002575263081386)
XLA Ops:
  0.0 103.8 %layers.1 = (bf16[8,32,2048]{2,1,0:T(8,128)(2,1)S(1)}, bf16[55296,512]{1,0:T(8,128)(2,1)S(1)}) custom-call(bf16[32,2048]{1,0:T(8,128)(2,1)} %x_hbm.1, s32[1,32]{1,0:T(1,128)} %bitcast.9, f32[2,2048]{1,0:T(2,128)} %gain_attn_hbm.1, f32[2,2048]{1,0:T(2,128)} %gain_ffn_hbm.1, f32[1,2048]{1,0:T(1,128)} %bitcast.8, bf16[2,32,576,512]{3,2,1,0:T(8,128)(2,1)} %bitcast.5, ...), custom_call_target="tpu_custom_call" | custom-call | tf_op jit(solution)/shard_map/layers/pallas_call | solution.py:430
  103.8 15.8 %head.1 = f32[256,12800]{1,0:T(8,128)} custom-call(bf16[8,32,2048]{2,1,0:T(8,128)(2,1)S(1)} %get-tuple-element.7.rows, bf16[55296,512]{1,0:T(8,128)(2,1)S(1)} %get-tuple-element.8.buf), custom_call_target="tpu_custom_call" | custom-call | tf_op jit(solution)/shard_map/head/pallas_call | solution.py:387

commit v8 on v7

--- a/solution.py
+++ b/solution.py
@@ -134,10 +134,10 @@
             copy.wait_recv()
         return every
 
-    start(wq_copy(0, n) for n in range(n_q))
     small = [pltpu.make_async_copy(src, dst, in_sem.at[i]) for i, (src, dst) in enumerate(
         ((x_hbm, x_cur), (gain_attn_hbm, gain_attn), (gain_ffn_hbm, gain_ffn), (gain_fin_hbm, gain_fin), (len_hbm, len_ref)))]
     start(small)
+    start(wq_copy(0, n) for n in range(n_q))
     for copy in small:
         copy.wait()
 
@@ -156,8 +156,6 @@
         both_rows = hrows[...].reshape(2 * n_rows, d_model)
         prev, q_copies = None, []
         bounds = [(i, min(i + 3, n_q)) for i in range(0, n_q, 3)]
-        if l == 0:
-            bounds[-1:] = [(n_q - 3, n_q - 1), (n_q - 1, n_q)]
         for first, stop in bounds:
             for n in range(first, stop):
                 wq_copy(l, n).wait()

time: 120 us -> 119 us (level)
  no operation moved by 1% of the time
where the time goes in v8:
time: 119 us
  Pallas kernels  119 us (100%)
    pallas_call x1, Pallas kernels, run_layers(): pl.pallas_call(functools.partial(layers_kernel, dims), out_shape=[pltpu.V...  103 us
    pallas_call x1, Pallas kernels, run_head(): pl.pallas_call(functools.partial(head_kernel, (d_model, vocab)), out_shap...  15.8 us

profile of v8, /device:TPU:0, one launch (start us, length us, event | category | flops | bytes accessed | tf_op | source)
XLA Modules:
  0.0 119.1 jit_solution(3864144968491359057)
XLA Ops:
  0.0 103.1 %layers.1 = (bf16[8,32,2048]{2,1,0:T(8,128)(2,1)S(1)}, bf16[55296,512]{1,0:T(8,128)(2,1)S(1)}) custom-call(bf16[32,2048]{1,0:T(8,128)(2,1)} %x_hbm.1, s32[1,32]{1,0:T(1,128)} %bitcast.9, f32[2,2048]{1,0:T(2,128)} %gain_attn_hbm.1, f32[2,2048]{1,0:T(2,128)} %gain_ffn_hbm.1, f32[1,2048]{1,0:T(1,128)} %bitcast.8, bf16[2,32,576,512]{3,2,1,0:T(8,128)(2,1)} %bitcast.5, ...), custom_call_target="tpu_custom_call" | custom-call | tf_op jit(solution)/shard_map/layers/pallas_call | solution.py:428
  103.1 15.8 %head.1 = f32[256,12800]{1,0:T(8,128)} custom-call(bf16[8,32,2048]{2,1,0:T(8,128)(2,1)S(1)} %get-tuple-element.7.rows, bf16[55296,512]{1,0:T(8,128)(2,1)S(1)} %get-tuple-element.8.buf), custom_call_target="tpu_custom_call" | custom-call | tf_op jit(solution)/shard_map/head/pallas_call | solution.py:385

commit v9 on v6

--- a/solution.py
+++ b/solution.py
@@ -150,15 +150,17 @@
         copy.wait_recv()
         both_rows = hrows[...].reshape(2 * n_rows, d_model)
         prev, q_copies = None, []
-        for first in range(0, n_q, 3):
-            for n in range(first, first + 3):
+        bounds = [(i, min(i + 3, n_q)) for i in range(0, n_q, 3)]
+        if l == 0:
+            bounds[-1:] = [(n_q - 3, n_q - 1), (n_q - 1, n_q)]
+        for first, stop in bounds:
+            for n in range(first, stop):
                 wq_copy(l, n).wait()
             if l == 0:
-                per = -(-3 * n_rows // n_q)
-                start(kv_copy(l, b) for b in range(first // 3 * per, min((first // 3 + 1) * per, n_rows)))
-            weights = jnp.concatenate([buf[wq_at(l, n * d_model, d_model), :] for n in range(first, first + 3)], axis=1)
+                start(kv_copy(l, b) for b in range(first * n_rows // n_q, stop * n_rows // n_q))
+            weights = jnp.concatenate([buf[wq_at(l, n * d_model, d_model), :] for n in range(first, stop)], axis=1)
             wide = dot(both_rows, weights).astype(BF16).astype(F32)
-            for n in range(first, first + 3):
+            for n in range(first, stop):
                 cur = wide[:, (n - first) * CHUNK:(n - first + 1) * CHUNK]
                 if n >= 1:
                     h = n - 1

time: 115 us -> 115 us (level)
  no operation moved by 1% of the time
where the time goes in v9:
time: 115 us
  Pallas kernels  115 us (100%)
    pallas_call x1, Pallas kernels, run_layers(): pl.pallas_call(functools.partial(layers_kernel, dims), out_shape=[pltpu.V...  98.9 us
    pallas_call x1, Pallas kernels, run_head(): pl.pallas_call(functools.partial(head_kernel, (d_model, vocab)), out_shap...  15.8 us

profile of v9, /device:TPU:0, one launch (start us, length us, event | category | flops | bytes accessed | tf_op | source)
XLA Modules:
  0.0 114.9 jit_solution(2326119703234436577)
XLA Ops:
  0.0 98.9 %layers.1 = (bf16[8,32,2048]{2,1,0:T(8,128)(2,1)S(1)}, bf16[55296,512]{1,0:T(8,128)(2,1)S(1)}) custom-call(bf16[32,2048]{1,0:T(8,128)(2,1)} %x_ref.1, s32[32]{0:T(128)} %len_ref.1, f32[2,2048]{1,0:T(2,128)} %gain_attn.1, f32[2,2048]{1,0:T(2,128)} %gain_ffn.1, f32[1,2048]{1,0:T(1,128)} %bitcast.7, bf16[2,32,576,512]{3,2,1,0:T(8,128)(2,1)} %bitcast.4, ...), custom_call_target="tpu_custom_call" | custom-call | tf_op jit(solution)/shard_map/layers/pallas_call | solution.py:424
  98.9 15.8 %head.1 = f32[256,12800]{1,0:T(8,128)} custom-call(bf16[8,32,2048]{2,1,0:T(8,128)(2,1)S(1)} %get-tuple-element.7.rows, bf16[55296,512]{1,0:T(8,128)(2,1)S(1)} %get-tuple-element.8.buf), custom_call_target="tpu_custom_call" | custom-call | tf_op jit(solution)/shard_map/head/pallas_call | solution.py:382
